TPU v7x, 256 devices: a whole 4x4x8 slice. The times are simulated.
256 devices in a mesh: dp: 4 (over y), expert: 16 (over z, core), pipe: 4 (over x).
Axes of the slice: x: 4, y: 4, z: 8, core: 2. Of those that a mesh axis runs over, the one named last changes fastest.
Arguments:
- inputs: bfloat16 [2048, 4096], P('expert'), may hold values from -6 to 6
- cotangents: bfloat16 [2048, 4096], P('expert'), may hold values from -6 to 6
- routes: int32 [2048, 2], P('expert'), may hold values from 0 to 15, all different within a row; in each aligned block of 128 rows (0 to 127, 128 to 255, ...) at most 32 rows name the same one
- gates: float32 [2048, 2], P('expert'), may hold values from 0.1 to 1
- w_gate: bfloat16 [16, 4096, 7168], P('expert', None, ('dp', 'pipe')), may hold values from -0.09375 to 0.09375
- w_up: bfloat16 [16, 4096, 7168], P('expert', None, ('dp', 'pipe')), may hold values from -0.09375 to 0.09375
- w_down: bfloat16 [16, 7168, 4096], P('expert', ('dp', 'pipe')), may hold values from -0.09375 to 0.09375
- proj_in: bfloat16 [4096, 32], replicated, may hold values from -0.09375 to 0.09375
- proj_out: bfloat16 [4096, 64], replicated, may hold values from -0.09375 to 0.09375
- proj_hid_a: bfloat16 [7168, 32], P(('dp', 'pipe')), may hold values from -0.0625 to 0.0625
- proj_hid_b: bfloat16 [7168, 64], P(('dp', 'pipe')), may hold values from -0.0625 to 0.0625
- queries: bfloat16 [256, 6144], P(('dp', 'pipe')), may hold values from -0.078125 to 0.078125
Outputs:
- token_scores: float32 [2048, 256], P('expert', ('dp', 'pipe'))
- query_totals: float32 [256], P(('dp', 'pipe'))
Inputs may be any that keep to these rules, and one draw needn't show every extreme that they name: `routes`: each row names two different experts. Among the 128 tokens of one index of expert (aligned blocks), no expert is named more than 32 times, and in some blocks one expert is named exactly 32 times.
All inputs are finite; a program needn't handle non-finite values.
Results may differ from a plain program's by a relative error of at most 0.0041.
Values may be sent and summed in bfloat16 or wider, within the bound.
A program may use at most 128 MiB of HBM per device.

v0:
```python
import math

import jax
import jax.numpy as jnp
from jax import lax
from jax.sharding import PartitionSpec as P


def sent_to_all(x, axis):
    count = lax.axis_size(axis)
    return lax.all_to_all(jnp.broadcast_to(x[None], (count, *x.shape)), axis, 0, 0, tiled=True)


def of_everyone(x, axis):
    return sent_to_all(x, axis).sum(axis=0)


def in_one(arrays, axis):
    vector, at, finished = (jnp.concatenate([a.reshape(-1) for a in arrays]), 0, [])
    so_far = of_everyone(vector, axis)
    for a in arrays:
        finished.append(so_far[at : at + a.size].reshape(a.shape))
        at += a.size
    return tuple(finished)


def in_one_piece(arrays, axis, split_dim, concat_dim, along):
    both = jnp.concatenate(arrays, axis=along)
    whole, at, finished = (
        lax.all_to_all(both, axis, split_axis=split_dim, concat_axis=concat_dim, tiled=True),
        0,
        [],
    )
    for a in arrays:
        finished.append(lax.slice_in_dim(whole, at, at + a.shape[along], axis=along))
        at += a.shape[along]
    return tuple(finished)


def sent_together(arrays, axis, dim, along):
    both = jnp.concatenate(arrays, axis=along)
    whole, at, finished = (lax.all_gather(both, axis, axis=dim, tiled=True), 0, [])
    for a in arrays:
        finished.append(lax.slice_in_dim(whole, at, at + a.shape[along], axis=along))
        at += a.shape[along]
    return tuple(finished)


def slot_matrix(route_rows, gate_rows, experts, capacity):
    count = route_rows.shape[0]
    flat = route_rows.reshape(-1)
    labels = jnp.arange(experts, dtype=jnp.int32)
    onehot = (flat[:, None] == labels[None, :]).astype(jnp.int32)
    earlier = jnp.cumsum(onehot, axis=0) - onehot
    position = jnp.sum(onehot * (labels[None, :] * capacity + earlier), axis=1)
    slot_ids = jnp.arange(experts * capacity, dtype=jnp.int32)
    table = (
        (position[None, :] == slot_ids[:, None])
        .astype(jnp.float32)
        .reshape(experts * capacity, count, 2)
    )
    picks = jnp.sum(table, axis=2)
    weighted = jnp.sum(table * gate_rows[None, :, :], axis=2)
    return (picks, weighted)


def send_back(scores):
    return lax.all_to_all(scores, "expert", split_axis=0, concat_axis=0, tiled=True)


def body(
    inputs,
    cotangents,
    routes,
    gates,
    w_gate,
    w_up,
    w_down,
    proj_in,
    proj_out,
    proj_hid_a,
    proj_hid_b,
    queries,
):
    experts = lax.axis_size("expert")
    count = inputs.shape[0]
    width = inputs.shape[1]
    capacity = 4 * count // experts
    query_count = queries.shape[0]
    gate_proj = w_gate[0]
    up_proj = w_up[0]
    down_proj = w_down[0]
    picks, weighted = slot_matrix(routes, gates, experts, capacity)
    pick_rows = picks.astype(jnp.bfloat16)
    columns = width // lax.axis_size(("dp", "pipe"))
    column_start = lax.axis_index(("dp", "pipe")) * columns
    part_in = lax.dynamic_slice_in_dim(inputs, column_start, columns, 1)
    part_back = lax.dynamic_slice_in_dim(cotangents, column_start, columns, 1)
    buffer_in = jnp.dot(pick_rows, part_in, preferred_element_type=jnp.float32).astype(jnp.bfloat16)
    buffer_back = jnp.dot(pick_rows, part_back, preferred_element_type=jnp.float32).astype(
        jnp.bfloat16
    )
    sent_in, sent_back = in_one_piece(
        (
            buffer_in.reshape(experts, capacity, columns),
            buffer_back.reshape(experts, capacity, columns),
        ),
        "expert",
        0,
        0,
        1,
    )
    full_in, full_back = sent_together((sent_in, sent_back), ("dp", "pipe"), 2, 0)
    slot_in = full_in.reshape(-1, width)
    gate_pre = jnp.dot(slot_in, gate_proj, preferred_element_type=jnp.float32)
    up_pre = jnp.dot(slot_in, up_proj, preferred_element_type=jnp.float32)
    sigma = jax.nn.sigmoid(gate_pre)
    hidden = (gate_pre * sigma * up_pre).astype(jnp.bfloat16)
    a_part = jnp.dot(hidden, proj_hid_a, preferred_element_type=jnp.float32)
    slot_back = full_back.reshape(-1, width)
    gate_pre, up_pre, sigma, a_part = (gate_pre, up_pre, sigma, a_part)
    back = lax.dot_general(
        slot_back, down_proj, (((1,), (1,)), ((), ())), preferred_element_type=jnp.float32
    )
    d_up = (back * gate_pre * sigma).astype(jnp.bfloat16)
    d_gate = (back * up_pre * sigma * (1.0 + gate_pre * (1.0 - sigma))).astype(jnp.bfloat16)
    b_up_part = jnp.dot(d_up, proj_hid_b, preferred_element_type=jnp.float32)
    b_gate_part = jnp.dot(d_gate, proj_hid_b, preferred_element_type=jnp.float32)
    a_hidden, b_up, b_gate = in_one((a_part, b_up_part, b_gate_part), ("dp", "pipe"))
    a_input = jnp.dot(slot_in, proj_in, preferred_element_type=jnp.float32)
    b_output = jnp.dot(slot_back, proj_out, preferred_element_type=jnp.float32)
    height = slot_in.shape[0]
    sketch = jnp.concatenate(
        [
            (a_hidden[:, :, None] * b_output[:, None, :]).reshape(height, -1),
            (a_input[:, :, None] * b_up[:, None, :]).reshape(height, -1),
            (a_input[:, :, None] * b_gate[:, None, :]).reshape(height, -1),
        ],
        axis=1,
    ).astype(jnp.bfloat16)
    scores = lax.dot_general(
        sketch, queries, (((1,), (1,)), ((), ())), preferred_element_type=jnp.float32
    )
    returned = send_back(scores.reshape(experts, capacity, query_count))
    token_scores = lax.dot_general(
        weighted,
        returned.reshape(-1, query_count),
        (((0,), (0,)), ((), ())),
        precision=lax.Precision.HIGHEST,
        preferred_element_type=jnp.float32,
    )
    scale = 1.0 / math.sqrt(count * experts)
    partial_sum = jnp.sum(token_scores, axis=0)
    totals = of_everyone(partial_sum, "expert")
    return (token_scores, totals * scale)


def solution(mesh):
    placed = (
        P("expert", None),
        P("expert", None),
        P("expert", None),
        P("expert", None),
        P("expert", None, ("dp", "pipe")),
        P("expert", None, ("dp", "pipe")),
        P("expert", ("dp", "pipe"), None),
        P(),
        P(),
        P(("dp", "pipe"), None),
        P(("dp", "pipe"), None),
        P(("dp", "pipe"), None),
    )
    return jax.shard_map(
        body,
        mesh=mesh,
        in_specs=placed,
        out_specs=(P("expert", ("dp", "pipe")), P(("dp", "pipe"))),
        check_vma=False,
    )
```

profile of v0, /device:TPU:1, one launch (start us, length us, event | category | flops | bytes accessed | tf_op | source)
XLA Modules:
  0.0 265.4 jit_solution(7318821364939937244)
XLA Ops:
  7.2 0.9 copy.62
  8.4 0.6 reduce-window.6
  9.5 0.8 convert_reduce_fusion
  10.4 0.2 convolution_convert_fusion
  10.6 1.0 convolution_convert_fusion.1
  11.7 27.0 %all_to_all.22 = bf16[16,64,256]{2,1,0:T(8,128)(2,1)S(1)} all-to-all(bf16[16,64,256]{2,1,0:T(8,128)(2,1)S(1)} %pad_maximum_fusion), channel_id=1, replica_groups=mesh['dp'=4,'expert'=16,'pipe'=4] {'expert'}, dimensions={0} | all-to-all | bytes 1048576 | tf_op jit(solution)/shard_map/all_to_all | solution.py:30
  38.7 0.9 pad_maximum_fusion.1
  39.6 77.8 %all-gather.2.cloned.1.call-done = bf16[32,32,4096]{2,1,0:T(8,128)(2,1)} async-done(((bf16[32,32,256]{2,1,0:T(8,128)(2,1)}), bf16[32,32,4096]{2,1,0:T(8,128)(2,1)}) %all-gather.2.cloned.1.call-update) | async-done | bytes 8388624 | tf_op jit(solution)/shard_map/all_gather | solution.py:42
  117.4 4.1 %fusion.30 = (bf16[16,32,4096]{2,1,0:T(8,128)(2,1)S(1)}, bf16[16,32,4096]{2,1,0:T(8,128)(2,1)S(1)}) fusion(bf16[32,32,4096]{2,1,0:T(8,128)(2,1)} %all-gather.2.cloned.1.call-done), kind=kLoop, calls=%fused_computation.52 | loop fusion | bytes 16777216 | tf_op jit(solution)/shard_map/slice | solution.py:44
  121.6 0.4 copy-done.6
  121.9 2.1 fusion.10
  124.0 2.4 copy-done.7
  126.5 2.1 fusion.8
  128.6 2.1 fusion.6
  130.7 0.5 fusion.12
  131.2 0.6 fusion.14
  131.9 0.5 fusion.13
  132.7 6.4 %broadcast_in_dim.4 = f32[16,1,81920]{2,1,0:T(1,128)} broadcast(f32[81920]{0:T(1024)S(1)} %pad_maximum_fusion.2), dimensions={2} | broadcast | bytes 5570560 | tf_op jit(solution)/shard_map/broadcast_in_dim | solution.py:11
  139.1 4.9 %all-to-all-start.1 = ((f32[16,1,81920]{2,1,0:T(1,128)}), f32[16,1,81920]{2,1,0:T(1,128)}, u32[]{:S(2)}, u32[]{:S(2)}) async-start(f32[16,1,81920]{2,1,0:T(1,128)} %broadcast_in_dim.4), calls=%async_computation.1 | async-start | bytes 10485760 | tf_op jit(solution)/shard_map/all_to_all | solution.py:11
  144.1 3.7 %fusion.35 = f32[512,32]{0,1:T(8,128)S(1)} fusion(bf16[512,4096]{1,0:T(8,128)(2,1)} %bitcast.67, bf16[4096,32]{0,1:T(8,128)(2,1)S(1)} %copy-done.5), kind=kOutput, calls=%fused_computation.58 | convolution fusion | flops 134217728 | bytes 4521984 | tf_op jit(solution)/shard_map/dot_general | solution.py:130
  147.8 1.4 fusion.34
  149.2 69.2 %all-to-all-done.1 = f32[16,1,81920]{2,1,0:T(1,128)} async-done(((f32[16,1,81920]{2,1,0:T(1,128)}), f32[16,1,81920]{2,1,0:T(1,128)}, u32[]{:S(2)}, u32[]{:S(2)}) %all-to-all-start.1) | async-done | bytes 5242912 | tf_op jit(solution)/shard_map/all_to_all | solution.py:11
  218.4 5.9 %reduce_sum.57 = f32[81920]{0:T(1024)S(1)} reduce(f32[16,1,81920]{2,1,0:T(1,128)} %all-to-all-done.1, f32[]{:T(128)} %constant.7.clone.1), dimensions={0,1}, to_apply=%region_5.6 | reduce | flops 1228800 | bytes 5570564 | tf_op jit(solution)/shard_map/reduce_sum | solution.py:15
  225.0 0.6 multiply_convert_fusion.2
  225.6 1.4 multiply_convert_fusion.1
  227.0 1.1 fusion
  228.3 17.3 %all_to_all.23 = f32[16,1,512]{2,1,0:T(1,128)S(1)} all-to-all(f32[16,1,512]{2,1,0:T(1,128)S(1)} %reshape.131), channel_id=1, replica_groups=mesh['dp'=4,'expert'=16,'pipe'=4] {'expert'}, dimensions={0} | all-to-all | bytes 65536 | tf_op jit(solution)/shard_map/all_to_all | solution.py:68
  245.6 0.5 broadcast.70
  246.2 0.7 reduce.4
  247.1 1.0 fusion.33
  248.1 9.9 %all_to_all.24 = f32[16,1,16]{2,1,0:T(1,128)S(1)} all-to-all(f32[16,1,16]{2,1,0:T(1,128)S(1)} %broadcast_in_dim.5), channel_id=1, replica_groups=mesh['dp'=4,'expert'=16,'pipe'=4] {'expert'}, dimensions={0} | all-to-all | bytes 2048 | tf_op jit(solution)/shard_map/all_to_all | solution.py:11
  258.0 0.5 broadcast_multiply_fusion
  (56 shorter events, 2.5 us)
Async XLA Ops:
  7.2 3.2 %copy-start = (bf16[128,4096]{1,0:T(8,128)(2,1)S(1)}, bf16[128,4096]{1,0:T(8,128)(2,1)}, u32[]{:S(2)}) copy-start(bf16[128,4096]{1,0:T(8,128)(2,1)} %param.13) | copy-start | bytes 3145732
  7.2 110.3 %all-gather.2.cloned.1.call-start = ((), (), s32[]{:S(2)}) async-start(), calls=%async_computation.4 | async-start | bytes 8912896 | tf_op jit(solution)/shard_map/all_gather | solution.py:42
  117.4 4.5 %copy-start.6 = (bf16[1,4096,448]{1,2,0:T(8,128)(2,1)S(1)}, bf16[1,4096,448]{1,2,0:T(8,128)(2,1)}, u32[]{:S(2)}) copy-start(bf16[1,4096,448]{1,2,0:T(8,128)(2,1)} %param.16) | copy-start | bytes 11010052
  121.6 2.5 copy-start.3
  121.6 7.0 %copy-start.1 = (bf16[16,32,4096]{2,1,0:T(8,128)(2,1)}, bf16[16,32,4096]{2,1,0:T(8,128)(2,1)S(1)}, u32[]{:S(2)}) copy-start(bf16[16,32,4096]{2,1,0:T(8,128)(2,1)S(1)} %get-tuple-element.4) | copy-start | bytes 12582916
  121.9 4.5 %copy-start.7 = (bf16[1,4096,448]{1,2,0:T(8,128)(2,1)S(1)}, bf16[1,4096,448]{1,2,0:T(8,128)(2,1)}, u32[]{:S(2)}) copy-start(bf16[1,4096,448]{1,2,0:T(8,128)(2,1)} %param.17) | copy-start | bytes 11010052
  126.5 2.1 copy-start.8
  128.6 2.1 copy-start.10
  130.7 1.2 copy-start.11
  139.1 4.9 %copy-start.5 = (bf16[4096,32]{0,1:T(8,128)(2,1)S(1)}, bf16[4096,32]{0,1:T(8,128)(2,1)}, u32[]{:S(2)}) copy-start(bf16[4096,32]{0,1:T(8,128)(2,1)} %param.19) | copy-start | bytes 786436
  139.1 8.6 %copy-start.4 = (bf16[4096,64]{0,1:T(8,128)(2,1)S(1)}, bf16[4096,64]{0,1:T(8,128)(2,1)}, u32[]{:S(2)}) copy-start(bf16[4096,64]{0,1:T(8,128)(2,1)} %param.20) | copy-start | bytes 1572868
  139.1 79.2 %all-to-all-start.1 = ((f32[16,1,81920]{2,1,0:T(1,128)}), f32[16,1,81920]{2,1,0:T(1,128)}, u32[]{:S(2)}, u32[]{:S(2)}) async-start(f32[16,1,81920]{2,1,0:T(1,128)} %broadcast_in_dim.4), calls=%async_computation.1 | async-start | bytes 10485760 | tf_op jit(solution)/shard_map/all_to_all | solution.py:11
  144.1 3.7 %copy-start.2 = (bf16[16,32,4096]{2,1,0:T(8,128)(2,1)S(1)}, bf16[16,32,4096]{2,1,0:T(8,128)(2,1)}, u32[]{:S(2)}) copy-start(bf16[16,32,4096]{2,1,0:T(8,128)(2,1)} %copy-done.1) | copy-start | bytes 12582916
  224.5 2.4 copy-start.9
Sparse Core Ops, SparseCore 0:
  39.8 77.6 all-gather.1
where the time goes:
time: 266 us; the launch traced here: 265 us
  waiting for transfers between devices  147 us (55%)
  blocking collectives  54.2 us (20%)
  local copies, waits for them, and re-layouts  16.9 us (6%)
  matrix products  16.3 us (6%)
  between operations  14.4 us (5%)
  other arithmetic  11.6 us (4%)
  starting transfers between devices  4.96 us (2%)
    all_gather x1, waiting for transfers between devices, sent_together(): lax.all_gather(both, axis, axis=dim, tiled=True)  77.8 us
    all_to_all x1, waiting for transfers between devices, sent_to_all(): lax.all_to_all(jnp.broadcast_to(x[None], (count, *x.shape)), axis, 0, 0,...  69.2 us
    all_to_all x1, blocking collectives, in_one_piece(): lax.all_to_all(both, axis, split_axis=split_dim, concat_axis=concat_dim,...  27 us
    all_to_all x1, blocking collectives, send_back(): lax.all_to_all(scores, 'expert', split_axis=0, concat_axis=0, tiled=True)  17.3 us
    all_to_all x1, blocking collectives, sent_to_all(): lax.all_to_all(jnp.broadcast_to(x[None], (count, *x.shape)), axis, 0, 0,...  9.87 us
    broadcast_in_dim x2, local copies, waits for them, and re-layouts, sent_to_all(): jnp.broadcast_to(x[None], (count, *x.shape))  6.4 us
    reduce_sum x2, other arithmetic, of_everyone(): return sent_to_all(x, axis).sum(axis=0)  5.9 us
  transfers between devices with their start and end apart: 2, of which 2 were waited for; matrix products, arithmetic and copies ran while one was open for 2% of the time, Pallas kernels for 0%

commit v1 on v0

v1 whole, which is shorter than its diff:
```python
import math

import jax
import jax.numpy as jnp
from jax import lax
from jax.experimental import pallas as pl
from jax.experimental.pallas import tpu as pltpu
from jax.sharding import PartitionSpec as P

MESH = pl.DeviceIdType.MESH
F32, BF16, I32 = jnp.float32, jnp.bfloat16, jnp.int32

NZ = 8
ORDER = (1, 7, 2, 6, 3, 5, 0, 4)
LOCAL = ORDER.index(0)
SLOTS = 32
COLS = 256
SHARES = 16
GROUPS = ((0, 4), (4, 4), (8, 4), (14, 2))
PLANE = sorted(
    ((dy, dx) for dy in range(4) for dx in range(4) if dy or dx),
    key=lambda o: min(o[0], 4 - o[0]) + min(o[1], 4 - o[1]),
)


def nn(a, b):
    return lax.dot_general(a, b, (((1,), (0,)), ((), ())), preferred_element_type=F32)


def nt(a, b):
    return lax.dot_general(a, b, (((1,), (1,)), ((), ())), preferred_element_type=F32)


def iota(shape, dim):
    return lax.broadcasted_iota(I32, shape, dim)


def split(v):
    high = v.astype(BF16)
    return high, (v - high.astype(F32)).astype(BF16)


def kernel(
    x_hbm, g_hbm, routes_hbm, gates_hbm, wg_hbm, wu_hbm, wd_hbm, pin_hbm, pout_hbm, pa_hbm, pb_hbm, q_hbm,
    tok_ref, tot_ref,
    xs, gs, routes, gates, wg, wu, wd, pa, pb, qs,
    full, out_rows, out_pair, acc0, acc1, acc2, keep_in, keep_out,
    pat, pbt1, pbt2, wq0, wq12, wm_hi, wm_lo, wrow, wrecv,
    part, gathered, own, factors, score_send, score_recv, tot_send, tot_recv,
    load_sem, z_send, z_recv, pair_send, pair_recv, w_send, w_recv,
    g_send, g_recv, rs_send, rs_recv, ag_send, ag_recv, sc_send, sc_recv, t_send, t_recv,
):
    y, e, x = lax.axis_index("dp"), lax.axis_index("expert"), lax.axis_index("pipe")
    z, c = lax.div(e, 2), lax.rem(e, 2)
    other = 1 - c
    me = y * 4 + x

    def device(yy, ee, xx):
        return {"dp": yy, "expert": ee, "pipe": xx}

    def column(pos, core):
        return device(y, lax.rem(z + ORDER[pos], NZ) * 2 + core, x)

    def back_column(pos, core):
        return device(y, lax.rem(z + NZ - ORDER[pos], NZ) * 2 + core, x)

    def plane(dy, dx):
        return device(lax.rem(y + dy, 4), e, lax.rem(x + dx, 4))

    def plane_index(dy, dx):
        return lax.rem(y + dy, 4) * 4 + lax.rem(x + dx, 4)

    sent = []

    def remote(src, dst, ss, rs, dev):
        copy = pltpu.make_async_remote_copy(
            src_ref=src, dst_ref=dst, send_sem=ss, recv_sem=rs, device_id=dev, device_id_type=MESH
        )
        copy.start()
        sent.append(copy)

    def arrived(dst, rs):
        pltpu.make_async_remote_copy(
            src_ref=dst, dst_ref=dst, send_sem=rs, recv_sem=rs, device_id=device(y, e, x), device_id_type=MESH
        ).wait_recv()

    barrier = pltpu.get_barrier_semaphore()
    for dy, dx in PLANE:
        pl.semaphore_signal(barrier, inc=1, device_id=plane(dy, dx), device_id_type=MESH)
    for pos in range(NZ):
        if pos == LOCAL:
            pl.semaphore_signal(barrier, inc=1, device_id=column(pos, other), device_id_type=MESH)
        else:
            for core in range(2):
                pl.semaphore_signal(barrier, inc=1, device_id=column(pos, core), device_id_type=MESH)

    loads = {}
    for i, (name, src, dst) in enumerate(
        (
            ("routes", routes_hbm, routes),
            ("gates", gates_hbm, gates),
            ("x", x_hbm, xs),
            ("g", g_hbm, gs),
            ("q", q_hbm, qs),
            ("pa", pa_hbm, pa),
            ("pb", pb_hbm, pb),
            ("pin", pin_hbm, wg.at[448:480]),
            ("pout", pout_hbm, wd.at[448:512]),
            ("wg", wg_hbm, wg.at[0:448]),
            ("wu", wu_hbm, wu),
            ("wd", wd_hbm, wd.at[0:448]),
        )
    ):
        loads[name] = pltpu.make_async_copy(src, dst, load_sem.at[i])
        loads[name].start()

    loads["routes"].wait()
    loads["gates"].wait()
    first, second = routes[0:1, :], routes[1:2, :]
    expert_rows = iota((16, 128), 0)
    named = ((expert_rows == first) | (expert_rows == second)).astype(F32)
    before = (iota((128, 128), 0) < iota((128, 128), 1)).astype(F32)
    earlier = nn(named.astype(BF16), before.astype(BF16))

    def places(route):
        slot = jnp.sum(jnp.where(expert_rows == route, earlier, 0.0), axis=0, keepdims=True).astype(I32)
        offset = ((route >> 1) - z) & (NZ - 1)
        pos = jnp.zeros_like(offset)
        for i, o in enumerate(ORDER):
            pos = jnp.where(offset == o, i, pos)
        block = pos * 2 + (route & 1)
        lane = block * 128 + ((pos & 1) * 2 + c) * 32 + slot
        return block * SLOTS + slot, lane

    place0, lane0 = places(first)
    place1, lane1 = places(second)

    def picks_of(start, count):
        rows = iota((count, 128), 0) + start
        return ((rows == place0) | (rows == place1)).astype(F32).astype(BF16)

    picks = picks_of(0, 512)
    shares = (y * 4 + x, x * 4 + y)
    for a, (name, source) in enumerate((("x", xs), ("g", gs))):
        loads[name].wait()
        columns = pl.ds(pl.multiple_of(shares[a] * COLS, COLS), COLS)
        rows = nn(picks, source[:, columns]).astype(BF16)
        out_rows[a] = rows.reshape(16, SLOTS, COLS)
    pair_picks = picks_of((2 * LOCAL + other) * SLOTS, SLOTS)
    for a, source in enumerate((xs, gs)):
        for p in range(SHARES):
            out_pair[a, p] = nn(pair_picks, source[:, p * COLS : (p + 1) * COLS]).astype(BF16)

    pl.semaphore_wait(barrier, 30)

    for pos in range(NZ):
        if pos == LOCAL:
            continue
        for a in range(2):
            for core in range(2):
                remote(
                    out_rows.at[a, 2 * pos + core],
                    full.at[a, shares[a], 2 * pos + c],
                    z_send.at[a, 2 * pos + core],
                    z_recv.at[a, 2 * pos + c],
                    column(pos, core),
                )
    for a in range(2):
        remote(
            out_pair.at[a],
            full.at[a, :, 2 * LOCAL + c],
            pair_send.at[a],
            pair_recv.at[a],
            device(y, z * 2 + other, x),
        )

    own_picks = picks_of((2 * LOCAL + c) * SLOTS, SLOTS)
    for a, source in enumerate((xs, gs)):
        for p in range(SHARES):
            full[a, p, 2 * LOCAL + c] = nn(own_picks, source[:, p * COLS : (p + 1) * COLS]).astype(BF16)

    lanes = iota((2048, 128), 0)
    weights = jnp.where(lanes == lane0, gates[0:1, :], 0.0) + jnp.where(lanes == lane1, gates[1:2, :], 0.0)
    high, low = split(weights)
    wm_hi[...] = high
    wm_lo[...] = low
    ones = jnp.ones((8, 128), BF16)
    sums = nt(ones, high) + nt(ones, low)
    for k in range(16):
        wrow[k] = sums[0:1, k * 128 : (k + 1) * 128]

    def ring(a, major, minor):
        major, minor = lax.rem(major + 4, 4), lax.rem(minor + 4, 4)
        return device(major, e, minor) if a == 0 else device(minor, e, major)

    mine = ((y, x), (x, y))

    def share_ref(a, dmajor, dminor, first_block, blocks):
        major, minor = mine[a]
        share = lax.rem(major + dmajor + 4, 4) * 4 + lax.rem(minor + dminor + 4, 4)
        return full.at[a, share, pl.ds(first_block, blocks)]

    def major_ref(a, dmajor, first_block, blocks):
        share = lax.rem(mine[a][0] + dmajor + 4, 4) * 4
        return full.at[a, pl.ds(share, 4), pl.ds(first_block, blocks)]

    def send_group(g, a, tag, ref, dmajor, dminor):
        major, minor = mine[a]
        remote(ref, ref, g_send.at[g, a, tag], g_recv.at[g, a, tag], ring(a, major + dmajor, minor + dminor))

    def step_a(g):
        b, n = GROUPS[g]
        for a in range(2):
            for i in range(n):
                arrived(full.at[a, shares[a], b + i], z_recv.at[a, b + i])
            for tag, d in ((0, 1), (1, -1)):
                send_group(g, a, tag, share_ref(a, 0, 0, b, n), 0, d)

    def step_b(g):
        b, n = GROUPS[g]
        h = n // 2
        for a in range(2):
            arrived(share_ref(a, 0, -1, b, n), g_recv.at[g, a, 0])
            send_group(g, a, 2, share_ref(a, 0, -1, b, h), 0, 1)
            arrived(share_ref(a, 0, 1, b, n), g_recv.at[g, a, 1])
            send_group(g, a, 3, share_ref(a, 0, 1, b + h, h), 0, -1)

    def step_c(g):
        b, n = GROUPS[g]
        h = n // 2
        for a in range(2):
            arrived(share_ref(a, 0, 2, b, h), g_recv.at[g, a, 2])
            arrived(share_ref(a, 0, 2, b + h, h), g_recv.at[g, a, 3])
            for tag, d in ((4, 1), (5, -1)):
                send_group(g, a, tag, major_ref(a, 0, b, n), d, 0)

    def step_d(g):
        b, n = GROUPS[g]
        h = n // 2
        for a in range(2):
            arrived(major_ref(a, -1, b, n), g_recv.at[g, a, 4])
            send_group(g, a, 6, major_ref(a, -1, b, h), 1, 0)
            arrived(major_ref(a, 1, b, n), g_recv.at[g, a, 5])
            send_group(g, a, 7, major_ref(a, 1, b + h, h), -1, 0)

    def step_e(g):
        b, n = GROUPS[g]
        h = n // 2
        for a in range(2):
            arrived(major_ref(a, 2, b, h), g_recv.at[g, a, 6])
            arrived(major_ref(a, 2, b + h, h), g_recv.at[g, a, 7])

    def rows_of(a, chunk, b0):
        return jnp.concatenate([full[a, chunk * 4 + i, b0 : b0 + 8].reshape(256, COLS) for i in range(4)], axis=1)

    def chunk_in(cg, chunk, begin):
        ks = pl.ds(pl.multiple_of(chunk * 1024, 1024), 1024)
        rows = rows_of(0, chunk, cg * 8)
        for acc, w in ((acc0, wg), (acc1, wu)):
            v = nt(rows, w[:, ks])
            acc[...] = v if begin else acc[...] + v

    def chunk_back(cg, chunk, begin):
        ks = pl.ds(pl.multiple_of(chunk * 1024, 1024), 1024)
        v = nt(rows_of(1, chunk, cg * 8), wd[:, ks])
        acc2[...] = v if begin else acc2[...] + v

    def chunks(cg, offset, begin):
        chunk_in(cg, lax.rem(y + offset, 4), begin)
        chunk_back(cg, lax.rem(x + offset, 4), begin)

    def activations(cg):
        gate, up, back = acc0[:, :448], acc1[...], acc2[:, :448]
        s = jax.nn.sigmoid(gate)
        gated = gate * s
        hidden = (gated * up).astype(BF16)
        d_up = (back * gated).astype(BF16)
        d_gate = (back * up * s * (1.0 + gate * (1.0 - s))).astype(BF16)
        sums = nt(d_up, pbt1[...]) + nt(d_gate, pbt2[...]) + nt(hidden, pat[...])
        part[cg] = sums.astype(BF16).reshape(16, 16, 256)
        keep_in[cg] = acc0[:, 384:512]
        keep_out[cg] = acc2[:, 384:512]

    def scatter(cg):
        for r, (dy, dx) in enumerate(PLANE):
            remote(
                part.at[cg, plane_index(dy, dx)],
                gathered.at[cg, me],
                rs_send.at[cg, r],
                rs_recv.at[cg, r],
                plane(dy, dx),
            )

    def gather(cg):
        total = part[cg, me].astype(F32)
        for r, (dy, dx) in enumerate(PLANE):
            source = plane_index(4 - dy, 4 - dx)
            arrived(gathered.at[cg, source], rs_recv.at[cg, r])
            total = total + gathered[cg, source].astype(F32)
        own[cg] = total.astype(BF16)
        for r, (dy, dx) in enumerate(PLANE):
            remote(own.at[cg], factors.at[cg, me], ag_send.at[cg, r], ag_recv.at[cg, r], plane(dy, dx))
        factors[cg, me] = total.astype(BF16)

    low_half = iota((256, 128), 1) < 64
    pairs = iota((128, 256), 1) // 16 * 2

    def picked(shift, odd):
        return (iota((128, 256), 0) == pairs + (shift + odd)).astype(F32).astype(BF16)

    def spread(values, odd):
        high, low = split(values)
        return nn(high, picked(64, odd)) + nn(low, picked(64, odd))

    def against(values, w):
        high, low = split(values)
        return nt(high, w) + nt(low, w)

    def scores(cg):
        for r, (dy, dx) in enumerate(PLANE):
            arrived(factors.at[cg, plane_index(4 - dy, 4 - dx)], ag_recv.at[cg, r])
        all_rows = factors[cg].reshape(256, 256)
        b_both = all_rows[:, :128].astype(F32)
        b_turned = pltpu.roll(b_both, 64, 1)
        b_out = keep_out[cg]
        out_turned = pltpu.roll(b_out, 64, 1)
        a_hidden, a_in = all_rows[:, 128:], keep_in[cg]
        even = jnp.concatenate([jnp.where(low_half, b_both, 0.0), jnp.where(low_half, b_turned, 0.0)], axis=1)
        odd = jnp.concatenate([jnp.where(low_half, 0.0, b_turned), jnp.where(low_half, 0.0, b_both)], axis=1)
        z_sum = spread(a_in, 0) * nt(even.astype(BF16), wq12[...])
        z_sum += spread(a_in, 1) * nt(odd.astype(BF16), wq12[...])
        z_sum += nn(a_hidden, picked(0, 0)) * against(jnp.where(low_half, out_turned, 0.0), wq0[...])
        z_sum += nn(a_hidden, picked(0, 1)) * against(jnp.where(low_half, 0.0, b_out), wq0[...])
        high, low = split(z_sum)
        fold = (lax.rem(iota((16, 256), 1), 16) == iota((16, 256), 0)).astype(F32).astype(BF16)
        score = nt(fold, high) + nt(fold, low)
        for t in range(2):
            score_send[cg, t] = score[:, t * 128 : (t + 1) * 128]
        for pos in range(cg * 4, cg * 4 + 4):
            tile = score_send.at[cg, (pos % 4) // 2]
            for core in range(2):
                if pos != LOCAL:
                    remote(
                        tile,
                        score_recv.at[2 * pos + c],
                        sc_send.at[2 * pos + core],
                        sc_recv.at[2 * pos + c],
                        back_column(pos, core),
                    )
            if pos == LOCAL:
                remote(
                    tile,
                    score_recv.at[2 * pos + c],
                    sc_send.at[2 * pos],
                    sc_recv.at[2 * pos + c],
                    device(y, z * 2 + other, x),
                )
                score_recv[2 * pos + c] = score_send[cg, (pos % 4) // 2]
        share = jnp.zeros((16, 128), F32)
        for t in range(2):
            w_tile = jnp.zeros((1, 128), F32)
            for k in range(4):
                w_tile = w_tile + wrecv[cg * 8 + t * 4 + k]
            share = share + score[:, t * 128 : (t + 1) * 128] * w_tile
        return jnp.sum(share, axis=1, keepdims=True)

    def constants():
        wg[480:512] = jnp.zeros((32, 4096), BF16)
        loads["q"].wait()
        for i in range(16):
            wq0[i * 16 : (i + 1) * 16, :] = qs[:, i * 128 : (i + 1) * 128]
            wq12[i * 16 : (i + 1) * 16, 0:128] = qs[:, 2048 + i * 128 : 2048 + (i + 1) * 128]
            wq12[i * 16 : (i + 1) * 16, 128:256] = qs[:, 4096 + i * 128 : 4096 + (i + 1) * 128]
        loads["pa"].wait()
        loads["pb"].wait()
        at = iota((256, 64), 0) - iota((256, 64), 1)
        pbt1[...] = nn((at == 0).astype(F32).astype(BF16), pb[...]).astype(BF16)
        pbt2[...] = nn((at == 64).astype(F32).astype(BF16), pb[...]).astype(BF16)
        at = iota((256, 32), 0) - iota((256, 32), 1)
        pat[...] = nn((at == 128).astype(F32).astype(BF16), pa[...]).astype(BF16)

    def send_weights():
        for pos in range(NZ):
            if pos == LOCAL:
                remote(
                    wrow.at[2 * pos + other],
                    wrecv.at[2 * pos + c],
                    w_send.at[2 * pos],
                    w_recv.at[2 * pos + c],
                    device(y, z * 2 + other, x),
                )
                wrecv[2 * pos + c] = wrow[2 * pos + c]
            else:
                for core in range(2):
                    remote(
                        wrow.at[2 * pos + core],
                        wrecv.at[2 * pos + c],
                        w_send.at[2 * pos + core],
                        w_recv.at[2 * pos + c],
                        column(pos, core),
                    )

    step_a(0)
    step_b(0)
    step_a(1)
    step_c(0)
    step_b(1)
    step_a(2)
    send_weights()
    step_d(0)
    step_c(1)
    step_b(2)
    step_a(3)
    constants()
    step_e(0)
    step_d(1)
    step_c(2)
    step_b(3)
    for name in ("pin", "pout", "wg", "wu", "wd"):
        loads[name].wait()
    step_e(1)
    chunks(0, 0, True)
    for offset in (1, 2):
        chunks(0, offset, False)
    step_d(2)
    step_c(3)
    chunks(0, 3, False)
    activations(0)
    scatter(0)
    for pos in range(NZ):
        for core in range(2):
            if pos != LOCAL:
                arrived(wrecv.at[2 * pos + core], w_recv.at[2 * pos + core])
    arrived(wrecv.at[2 * LOCAL + other], w_recv.at[2 * LOCAL + other])
    for a in range(2):
        arrived(full.at[a, :, 2 * LOCAL + other], pair_recv.at[a])
    chunks(1, 0, True)
    step_d(3)
    gather(0)
    step_e(2)
    chunks(1, 1, False)
    chunks(1, 3, False)
    total0 = scores(0)
    step_e(3)
    chunks(1, 2, False)
    activations(1)
    scatter(1)
    gather(1)
    total = total0 + scores(1)

    on_diagonal = iota((16, 128), 0) == iota((16, 128), 1)
    row = jnp.sum(jnp.where(on_diagonal, total, 0.0), axis=0, keepdims=True)
    tot_send[...] = row
    tot_recv[2 * LOCAL + c] = row
    for pos in range(NZ):
        for core in range(2):
            if pos != LOCAL:
                k = 2 * pos + core
                remote(tot_send, tot_recv.at[2 * pos + c], t_send.at[k], t_recv.at[2 * pos + c], back_column(pos, core))
    remote(
        tot_send,
        tot_recv.at[2 * LOCAL + c],
        t_send.at[2 * LOCAL],
        t_recv.at[2 * LOCAL + c],
        device(y, z * 2 + other, x),
    )

    def wait_all(buffer, sems):
        for pos in range(NZ):
            for core in range(2):
                if pos != LOCAL:
                    arrived(buffer.at[2 * pos + core], sems.at[2 * pos + core])
        arrived(buffer.at[2 * LOCAL + other], sems.at[2 * LOCAL + other])

    wait_all(score_recv, sc_recv)
    every = jnp.concatenate([score_recv[k] for k in range(16)], axis=1)
    high, low = split(every)
    tok_ref[...] = nn(high, wm_hi[...]) + nn(high, wm_lo[...]) + nn(low, wm_hi[...])
    wait_all(tot_recv, t_recv)
    row = tot_recv[0]
    for k in range(1, 16):
        row = row + tot_recv[k]
    tot_ref[...] = row[:, :16] * (1.0 / math.sqrt(2048.0))
    for copy in sent:
        copy.wait_send()


def body(inputs, cotangents, routes, gates, w_gate, w_up, w_down, proj_in, proj_out, proj_hid_a, proj_hid_b, queries):
    anywhere = pl.BlockSpec(memory_space=pl.ANY)
    vmem = pl.BlockSpec(memory_space=pltpu.VMEM)
    scores, totals = pl.pallas_call(
        kernel,
        out_shape=(jax.ShapeDtypeStruct((16, 128), F32), jax.ShapeDtypeStruct((1, 16), F32)),
        in_specs=[anywhere] * 12,
        out_specs=(vmem, vmem),
        scratch_shapes=[
            pltpu.VMEM((128, 4096), BF16),
            pltpu.VMEM((128, 4096), BF16),
            pltpu.VMEM((2, 128), I32),
            pltpu.VMEM((2, 128), F32),
            pltpu.VMEM((512, 4096), BF16),
            pltpu.VMEM((448, 4096), BF16),
            pltpu.VMEM((512, 4096), BF16),
            pltpu.VMEM((32, 448), BF16),
            pltpu.VMEM((64, 448), BF16),
            pltpu.VMEM((16, 6144), BF16),
            pltpu.VMEM((2, SHARES, 16, SLOTS, COLS), BF16),
            pltpu.VMEM((2, 16, SLOTS, COLS), BF16),
            pltpu.VMEM((2, SHARES, SLOTS, COLS), BF16),
            pltpu.VMEM((256, 512), F32),
            pltpu.VMEM((256, 448), F32),
            pltpu.VMEM((256, 512), F32),
            pltpu.VMEM((2, 256, 128), F32),
            pltpu.VMEM((2, 256, 128), F32),
            pltpu.VMEM((256, 448), BF16),
            pltpu.VMEM((256, 448), BF16),
            pltpu.VMEM((256, 448), BF16),
            pltpu.VMEM((256, 128), BF16),
            pltpu.VMEM((256, 256), BF16),
            pltpu.VMEM((2048, 128), BF16),
            pltpu.VMEM((2048, 128), BF16),
            pltpu.VMEM((16, 1, 128), F32),
            pltpu.VMEM((16, 1, 128), F32),
            pltpu.VMEM((2, 16, 16, 256), BF16),
            pltpu.VMEM((2, 16, 16, 256), BF16),
            pltpu.VMEM((2, 16, 256), BF16),
            pltpu.VMEM((2, 16, 16, 256), BF16),
            pltpu.VMEM((2, 2, 16, 128), F32),
            pltpu.VMEM((16, 16, 128), F32),
            pltpu.VMEM((1, 128), F32),
            pltpu.VMEM((16, 1, 128), F32),
            pltpu.SemaphoreType.DMA((12,)),
            pltpu.SemaphoreType.DMA((2, 16)),
            pltpu.SemaphoreType.DMA((2, 16)),
            pltpu.SemaphoreType.DMA((2,)),
            pltpu.SemaphoreType.DMA((2,)),
            pltpu.SemaphoreType.DMA((16,)),
            pltpu.SemaphoreType.DMA((16,)),
            pltpu.SemaphoreType.DMA((4, 2, 8)),
            pltpu.SemaphoreType.DMA((4, 2, 8)),
            pltpu.SemaphoreType.DMA((2, 15)),
            pltpu.SemaphoreType.DMA((2, 15)),
            pltpu.SemaphoreType.DMA((2, 15)),
            pltpu.SemaphoreType.DMA((2, 15)),
            pltpu.SemaphoreType.DMA((16,)),
            pltpu.SemaphoreType.DMA((16,)),
            pltpu.SemaphoreType.DMA((16,)),
            pltpu.SemaphoreType.DMA((16,)),
        ],
        compiler_params=pltpu.CompilerParams(
            collective_id=0, has_side_effects=True, vmem_limit_bytes=60 * 1024 * 1024
        ),
    )(
        inputs,
        cotangents,
        routes.T,
        gates.T,
        w_gate[0].T,
        w_up[0].T,
        w_down[0],
        proj_in.T,
        proj_out.T,
        proj_hid_a.T,
        proj_hid_b.T,
        queries,
    )
    return scores.T, totals.reshape(16)


def solution(mesh):
    placed = (
        P("expert", None),
        P("expert", None),
        P("expert", None),
        P("expert", None),
        P("expert", None, ("dp", "pipe")),
        P("expert", None, ("dp", "pipe")),
        P("expert", ("dp", "pipe"), None),
        P(),
        P(),
        P(("dp", "pipe"), None),
        P(("dp", "pipe"), None),
        P(("dp", "pipe"), None),
    )
    return jax.shard_map(
        body,
        mesh=mesh,
        in_specs=placed,
        out_specs=(P("expert", ("dp", "pipe")), P(("dp", "pipe"))),
        check_vma=False,
    )
```

time: 266 us -> 94.2 us (0.35)
  waiting for transfers between devices: 147 us -> 0 us
  Pallas kernels: 0 us -> 90.9 us
  blocking collectives: 54.2 us -> 0 us
  matrix products: 16.3 us -> 0 us
  local copies, waits for them, and re-layouts: 16.9 us -> 2.43 us
  between operations: 14.4 us -> 0.64 us
  other arithmetic: 11.6 us -> 0 us
  starting transfers between devices: 4.96 us -> 0 us
    pallas_call x0 -> x1, Pallas kernels: none -> 90.9 us  [body(): pl.pallas_call(kernel, out_shape=(jax.ShapeDtypeStruct((16, 128), F32), j...]
    all_gather x1 -> x0, waiting for transfers between devices: 77.8 us -> none  [sent_together(): lax.all_gather(both, axis, axis=dim, tiled=True)]
    all_to_all x1 -> x0, waiting for transfers between devices: 69.2 us -> none  [sent_to_all(): lax.all_to_all(jnp.broadcast_to(x[None], (count, *x.shape)), axis, 0, 0,...]
    all_to_all x3 -> x0, blocking collectives: 54.2 us -> none  [the longest x1 27 us: in_one_piece(): lax.all_to_all(both, axis, split_axis=split_dim, concat_axis=concat_dim,...]
    dot_general x12 -> x0, matrix products: 16.3 us -> none  [the longest x1 3.69 us: body(): a_input = jnp.dot(slot_in, proj_in, preferred_element_type=jnp.float32)]
    reduce_sum x4 -> x0, other arithmetic: 6.82 us -> none  [the longest x2 5.9 us: of_everyone(): return sent_to_all(x, axis).sum(axis=0)]
    broadcast_in_dim x2 -> x0, local copies, waits for them, and re-layouts: 6.4 us -> none  [sent_to_all(): jnp.broadcast_to(x[None], (count, *x.shape))]
    slice x11 -> x0, local copies, waits for them, and re-layouts: 4.99 us -> none  [the longest x1 4.1 us: sent_together(): lax.slice_in_dim(whole, at, at + a.shape[along], axis=along)]
  transfers between devices with their start and end apart: 2 -> 0, of which waited for: 2 -> 0; matrix products, arithmetic and copies ran while one was open for 2% -> 0% of each run, Pallas kernels for 0% -> 0%
where the time goes in v1:
time: 94.2 us; the launch traced here: 94 us
  Pallas kernels  90.9 us (96%)
  local copies, waits for them, and re-layouts  2.43 us (3%)
    pallas_call x1, Pallas kernels, body(): pl.pallas_call(kernel, out_shape=(jax.ShapeDtypeStruct((16, 128), F32), j...  90.9 us
    unnamed x2, local copies, waits for them, and re-layouts  2.43 us

profile of v1, /device:TPU:1, one launch (start us, length us, event | category | flops | bytes accessed | tf_op | source)
XLA Modules:
  0.0 94.0 jit_solution(11656404487271765752)
XLA Ops:
  0.6 90.9 %shard_map.131 = (f32[16,128]{1,0:T(8,128)}, f32[1,16]{1,0:T(1,128)}) custom-call(bf16[128,4096]{1,0:T(8,128)(2,1)} %x_hbm.1, bf16[128,4096]{1,0:T(8,128)(2,1)} %g_hbm.1, s32[2,128]{1,0:T(2,128)} %bitcast.23, f32[2,128]{1,0:T(2,128)} %bitcast.24, bf16[448,4096]{1,0:T(8,128)(2,1)} %bitcast.15, bf16[448,4096]{1,0:T(8,128)(2,1)} %bitcast.16, ...), custom_call_target="tpu_custom_call" | custom-call | tf_op jit(solution)/shard_map/pallas_call | solution.py:491
  91.6 1.3 %copy.16 = f32[128,16]{0,1:T(8,128)} copy(f32[128,16]{0,1:T(8,128)} %bitcast.22) | data formatting | bytes 16384
  92.9 1.1 %copy.17 = f32[16]{0:T(128)} copy(f32[16]{0:T(128)} %bitcast.25) | data formatting | bytes 128

commit v2 on v1

v2 whole, which is shorter than its diff:
```python
import math

import jax
import jax.numpy as jnp
from jax import lax
from jax.experimental import pallas as pl
from jax.experimental.pallas import tpu as pltpu
from jax.sharding import PartitionSpec as P

MESH = pl.DeviceIdType.MESH
F32, BF16, I32 = jnp.float32, jnp.bfloat16, jnp.int32

NZ = 8
ORDER = (2, 6, 3, 5, 4, 0, 1, 7)
LOCAL = ORDER.index(0)
NEAR = 6
SLOTS = 32
COLS = 256
SHARES = 16
GROUPS = ((0, 4), (4, 4), (8, 2))
PIECES = (0, -1, 1, 2)
PLANE = sorted(
    ((dy, dx) for dy in range(4) for dx in range(4) if dy or dx),
    key=lambda o: min(o[0], 4 - o[0]) + min(o[1], 4 - o[1]),
)


def nn(a, b):
    return lax.dot_general(a, b, (((1,), (0,)), ((), ())), preferred_element_type=F32)


def nt(a, b):
    return lax.dot_general(a, b, (((1,), (1,)), ((), ())), preferred_element_type=F32)


def iota(shape, dim):
    return lax.broadcasted_iota(I32, shape, dim)


def split(v):
    high = v.astype(BF16)
    return high, (v - high.astype(F32)).astype(BF16)


def kernel(
    x_hbm, g_hbm, routes_hbm, gates_hbm, wg_hbm, wu_hbm, wd_hbm, pin_hbm, pout_hbm, pa_hbm, pb_hbm, q_hbm,
    tok_ref, tot_ref,
    xs, gs, routes, gates, wg, wu, wd, pa, pb, qs,
    full, out_rows, out_pair, out_near, acc0, acc1, acc2, terms,
    pat, pbt1, pbt2, wq0, wq12, wm_hi, wm_lo, wrow, wrecv,
    part, gathered, own, factors, score_send, score_recv, tot_send, tot_recv,
    load_sem, z_send, z_recv, pair_recv, near_recv, w_send, w_recv,
    g_send, g_recv, e_recv, rs_send, rs_recv, ag_send, ag_recv, sc_send, sc_recv, t_send, t_recv,
):
    y, e, x = lax.axis_index("dp"), lax.axis_index("expert"), lax.axis_index("pipe")
    z, c = lax.div(e, 2), lax.rem(e, 2)
    other = 1 - c
    me = y * 4 + x

    def device(yy, ee, xx):
        return {"dp": yy, "expert": ee, "pipe": xx}

    def column(pos, core):
        return device(y, lax.rem(z + ORDER[pos], NZ) * 2 + core, x)

    def back_column(pos, core):
        return device(y, lax.rem(z + NZ - ORDER[pos], NZ) * 2 + core, x)

    def plane(dy, dx):
        return device(lax.rem(y + dy, 4), e, lax.rem(x + dx, 4))

    def plane_index(dy, dx):
        return lax.rem(y + dy, 4) * 4 + lax.rem(x + dx, 4)

    def remote(src, dst, ss, rs, dev):
        pltpu.make_async_remote_copy(
            src_ref=src, dst_ref=dst, send_sem=ss, recv_sem=rs, device_id=dev, device_id_type=MESH
        ).start()

    def arrived(dst, rs):
        pltpu.make_async_remote_copy(
            src_ref=dst, dst_ref=dst, send_sem=rs, recv_sem=rs, device_id=device(y, e, x), device_id_type=MESH
        ).wait_recv()

    def left(src, ss):
        pltpu.make_async_remote_copy(
            src_ref=src, dst_ref=src, send_sem=ss, recv_sem=ss, device_id=device(y, e, x), device_id_type=MESH
        ).wait_send()

    barrier = pltpu.get_barrier_semaphore()
    for dy, dx in PLANE:
        pl.semaphore_signal(barrier, inc=1, device_id=plane(dy, dx), device_id_type=MESH)
    for pos in range(NZ):
        if pos == LOCAL:
            pl.semaphore_signal(barrier, inc=1, device_id=column(pos, other), device_id_type=MESH)
        else:
            for core in range(2):
                pl.semaphore_signal(barrier, inc=1, device_id=column(pos, core), device_id_type=MESH)

    loads = {}
    for i, (name, src, dst) in enumerate(
        (
            ("routes", routes_hbm, routes),
            ("gates", gates_hbm, gates),
            ("x", x_hbm, xs),
            ("g", g_hbm, gs),
            ("q", q_hbm, qs),
            ("pa", pa_hbm, pa),
            ("pb", pb_hbm, pb),
            ("pin", pin_hbm, wg.at[448:480]),
            ("pout", pout_hbm, wd.at[448:512]),
            ("wg", wg_hbm, wg.at[0:448]),
            ("wu", wu_hbm, wu),
            ("wd", wd_hbm, wd.at[0:448]),
        )
    ):
        loads[name] = pltpu.make_async_copy(src, dst, load_sem.at[i])
        loads[name].start()

    loads["routes"].wait()
    loads["gates"].wait()
    first, second = routes[0:1, :], routes[1:2, :]
    expert_rows = iota((16, 128), 0)
    named = ((expert_rows == first) | (expert_rows == second)).astype(F32)
    before = (iota((128, 128), 0) < iota((128, 128), 1)).astype(F32)
    earlier = nn(named.astype(BF16), before.astype(BF16))

    def places(route):
        slot = jnp.sum(jnp.where(expert_rows == route, earlier, 0.0), axis=0, keepdims=True).astype(I32)
        offset = ((route >> 1) - z) & (NZ - 1)
        pos = jnp.zeros_like(offset)
        for i, o in enumerate(ORDER):
            pos = jnp.where(offset == o, i, pos)
        block = pos * 2 + (route & 1)
        lane = block * 128 + ((pos & 1) * 2 + c) * 32 + slot
        return block * SLOTS + slot, lane

    place0, lane0 = places(first)
    place1, lane1 = places(second)

    def picks_of(start, count):
        rows = iota((count, 128), 0) + start
        return ((rows == place0) | (rows == place1)).astype(F32).astype(BF16)

    far = 10 * SLOTS
    picks = picks_of(0, far)
    shares = (y * 4 + x, x * 4 + y)
    for a, (name, source) in enumerate((("x", xs), ("g", gs))):
        loads[name].wait()
        columns = pl.ds(pl.multiple_of(shares[a] * COLS, COLS), COLS)
        rows = nn(picks, source[:, columns]).astype(BF16)
        out_rows[a] = rows.reshape(10, SLOTS, COLS)

    pl.semaphore_wait(barrier, 30)

    def send_far(*positions):
        for pos in positions:
            for a in range(2):
                for core in range(2):
                    remote(
                        out_rows.at[a, 2 * pos + core],
                        full.at[a, shares[a], 2 * pos + c],
                        z_send,
                        z_recv.at[pos // 2, a],
                        column(pos, core),
                    )

    send_far(0, 1)

    near_picks = picks_of(2 * NEAR * SLOTS, 4 * SLOTS)
    for a, source in enumerate((xs, gs)):
        for p in range(SHARES):
            rows = nn(near_picks, source[:, p * COLS : (p + 1) * COLS]).astype(BF16)
            out_near[a, :, p] = rows.reshape(4, SLOTS, COLS)

    def send_near():
        for a in range(2):
            for core in range(2):
                for pos in range(NEAR, NZ):
                    k = 2 * (pos - NEAR)
                    remote(
                        out_near.at[a, k + core],
                        full.at[a, :, 2 * pos + c],
                        z_send,
                        near_recv,
                        column(pos, core),
                    )

    def chip_rows():
        pair_picks = picks_of((2 * LOCAL + other) * SLOTS, SLOTS)
        own_picks = picks_of((2 * LOCAL + c) * SLOTS, SLOTS)
        for a, source in enumerate((xs, gs)):
            for p in range(SHARES):
                columns = source[:, p * COLS : (p + 1) * COLS]
                out_pair[a, p] = nn(pair_picks, columns).astype(BF16)
                full[a, p, 2 * LOCAL + c] = nn(own_picks, columns).astype(BF16)

    def send_pair():
        for a in range(2):
            remote(
                out_pair.at[a],
                full.at[a, :, 2 * LOCAL + c],
                z_send,
                pair_recv,
                device(y, z * 2 + other, x),
            )

    def slot_weights():
        lanes = iota((2048, 128), 0)
        weights = jnp.where(lanes == lane0, gates[0:1, :], 0.0) + jnp.where(lanes == lane1, gates[1:2, :], 0.0)
        high, low = split(weights)
        wm_hi[...] = high
        wm_lo[...] = low
        ones = jnp.ones((8, 128), BF16)
        sums = nt(ones, high) + nt(ones, low)
        for k in range(16):
            wrow[k] = sums[0:1, k * 128 : (k + 1) * 128]

    def ring(a, major, minor):
        major, minor = lax.rem(major + 4, 4), lax.rem(minor + 4, 4)
        return device(major, e, minor) if a == 0 else device(minor, e, major)

    mine = ((y, x), (x, y))

    def share_ref(a, dmajor, dminor, first_block, blocks):
        major, minor = mine[a]
        share = lax.rem(major + dmajor + 4, 4) * 4 + lax.rem(minor + dminor + 4, 4)
        return full.at[a, share, pl.ds(first_block, blocks)]

    def send_group(a, ref, sem, dmajor, dminor):
        major, minor = mine[a]
        remote(ref, ref, g_send, sem, ring(a, major + dmajor, minor + dminor))

    def send_piece(g, a, piece):
        b, n = GROUPS[g]
        for way, d in enumerate((1, -1)):
            send_group(a, share_ref(a, 0, PIECES[piece], b, n), g_recv.at[g, a, 3 + 2 * piece + way], d, 0)

    def step_a(g):
        b, n = GROUPS[g]
        for a in range(2):
            arrived(share_ref(a, 0, 0, b, n), z_recv.at[g, a])
            for tag, d in ((0, 1), (1, -1)):
                send_group(a, share_ref(a, 0, 0, b, n), g_recv.at[g, a, tag], 0, d)
        if g == 0:
            for a in range(2):
                send_piece(g, a, 0)

    def step_b(g):
        b, n = GROUPS[g]
        h = n // 2
        for a in range(2):
            arrived(share_ref(a, 0, -1, b, n), g_recv.at[g, a, 0])
            send_group(a, share_ref(a, 0, -1, b, h), g_recv.at[g, a, 2], 0, 1)
            arrived(share_ref(a, 0, 1, b, n), g_recv.at[g, a, 1])
            send_group(a, share_ref(a, 0, 1, b + h, h), g_recv.at[g, a, 2], 0, -1)
        for a in range(2):
            for piece in (1, 2) if g == 0 else (0, 1, 2):
                send_piece(g, a, piece)

    def step_c(g):
        b, n = GROUPS[g]
        for a in range(2):
            arrived(share_ref(a, 0, 2, b, n), g_recv.at[g, a, 2])
            send_piece(g, a, 3)

    def step_d(g, *pieces):
        b, n = GROUPS[g]
        h = n // 2
        for piece in pieces:
            dm, tag = PIECES[piece], 3 + 2 * piece
            for a in range(2):
                arrived(share_ref(a, -1, dm, b, n), g_recv.at[g, a, tag])
                send_group(a, share_ref(a, -1, dm, b, h), e_recv.at[g], 1, 0)
                arrived(share_ref(a, 1, dm, b, n), g_recv.at[g, a, tag + 1])
                send_group(a, share_ref(a, 1, dm, b + h, h), e_recv.at[g], -1, 0)

    def step_e(g):
        b, n = GROUPS[g]
        arrived(full.at[:, 0:4, pl.ds(b, n)], e_recv.at[g])

    def rows_of(a, chunk, b0):
        return jnp.concatenate([full[a, chunk * 4 + i, b0 : b0 + 8].reshape(256, COLS) for i in range(4)], axis=1)

    def chunk_in(cg, chunk, begin):
        ks = pl.ds(pl.multiple_of(chunk * 1024, 1024), 1024)
        rows = rows_of(0, chunk, cg * 8)
        for acc, w in ((acc0, wg), (acc1, wu)):
            v = nt(rows, w[:, ks])
            acc[cg] = v if begin else acc[cg] + v

    def chunk_back(cg, chunk, begin):
        ks = pl.ds(pl.multiple_of(chunk * 1024, 1024), 1024)
        v = nt(rows_of(1, chunk, cg * 8), wd[:, ks])
        acc2[cg] = v if begin else acc2[cg] + v

    def chunks(cg, offset, begin):
        chunk_in(cg, lax.rem(y + offset, 4), begin)
        chunk_back(cg, lax.rem(x + offset, 4), begin)

    def activations(cg):
        gate, up, back = acc0[cg, :, :448], acc1[cg], acc2[cg, :, :448]
        s = jax.nn.sigmoid(gate)
        gated = gate * s
        hidden = (gated * up).astype(BF16)
        d_up = (back * gated).astype(BF16)
        d_gate = (back * up * s * (1.0 + gate * (1.0 - s))).astype(BF16)
        sums = nt(d_up, pbt1[...]) + nt(d_gate, pbt2[...]) + nt(hidden, pat[...])
        part[cg] = sums.astype(BF16).reshape(16, 16, 256)

    def scatter(cg):
        for dy, dx in PLANE:
            remote(
                part.at[cg, plane_index(dy, dx)],
                gathered.at[cg, me],
                rs_send.at[cg],
                rs_recv.at[cg],
                plane(dy, dx),
            )

    def gather(cg):
        total = part[cg, me].astype(F32)
        arrived(gathered.at[cg, 0:15], rs_recv.at[cg])
        for dy, dx in PLANE:
            total = total + gathered[cg, plane_index(dy, dx)].astype(F32)
        own[cg] = total.astype(BF16)
        for dy, dx in PLANE:
            remote(own.at[cg], factors.at[cg, me], ag_send.at[cg], ag_recv.at[cg], plane(dy, dx))
        factors[cg, me] = total.astype(BF16)

    low_half = iota((256, 128), 1) < 64
    pairs = iota((128, 256), 1) // 16 * 2

    def picked(shift, odd):
        return (iota((128, 256), 0) == pairs + (shift + odd)).astype(F32).astype(BF16)

    def spread(values, odd):
        high, low = split(values)
        return nn(high, picked(64, odd)) + nn(low, picked(64, odd))

    def against(values, w):
        high, low = split(values)
        return nt(high, w) + nt(low, w)

    def local_terms(cg):
        a_in, b_out = acc0[cg, :, 384:512], acc2[cg, :, 384:512]
        out_turned = pltpu.roll(b_out, 64, 1)
        terms[cg, 0] = spread(a_in, 0)
        terms[cg, 1] = spread(a_in, 1)
        terms[cg, 2] = against(jnp.where(low_half, out_turned, 0.0), wq0[...])
        terms[cg, 3] = against(jnp.where(low_half, 0.0, b_out), wq0[...])

    def scores(cg):
        arrived(factors.at[cg, 0:15], ag_recv.at[cg])
        all_rows = factors[cg].reshape(256, 256)
        b_both = all_rows[:, :128].astype(F32)
        b_turned = pltpu.roll(b_both, 64, 1)
        a_hidden = all_rows[:, 128:]
        even = jnp.concatenate([jnp.where(low_half, b_both, 0.0), jnp.where(low_half, b_turned, 0.0)], axis=1)
        odd = jnp.concatenate([jnp.where(low_half, 0.0, b_turned), jnp.where(low_half, 0.0, b_both)], axis=1)
        z_sum = terms[cg, 0] * nt(even.astype(BF16), wq12[...])
        z_sum += terms[cg, 1] * nt(odd.astype(BF16), wq12[...])
        z_sum += nn(a_hidden, picked(0, 0)) * terms[cg, 2]
        z_sum += nn(a_hidden, picked(0, 1)) * terms[cg, 3]
        high, low = split(z_sum)
        fold = (lax.rem(iota((16, 256), 1), 16) == iota((16, 256), 0)).astype(F32).astype(BF16)
        score = nt(fold, high) + nt(fold, low)
        for t in range(2):
            score_send[cg, t] = score[:, t * 128 : (t + 1) * 128]
        for pos in range(cg * 4, cg * 4 + 4):
            tile = score_send.at[cg, (pos % 4) // 2]
            for core in range(2):
                if pos != LOCAL:
                    remote(
                        tile,
                        score_recv.at[2 * pos + c],
                        sc_send,
                        sc_recv,
                        back_column(pos, core),
                    )
            if pos == LOCAL:
                remote(
                    tile,
                    score_recv.at[2 * pos + c],
                    sc_send,
                    sc_recv,
                    device(y, z * 2 + other, x),
                )
                score_recv[2 * pos + c] = score_send[cg, (pos % 4) // 2]
        share = jnp.zeros((16, 128), F32)
        for t in range(2):
            w_tile = jnp.zeros((1, 128), F32)
            for k in range(4):
                w_tile = w_tile + wrecv[cg * 8 + t * 4 + k]
            share = share + score[:, t * 128 : (t + 1) * 128] * w_tile
        return jnp.sum(share, axis=1, keepdims=True)

    def constants():
        wg[480:512] = jnp.zeros((32, 4096), BF16)
        loads["q"].wait()
        for i in range(16):
            wq0[i * 16 : (i + 1) * 16, :] = qs[:, i * 128 : (i + 1) * 128]
            wq12[i * 16 : (i + 1) * 16, 0:128] = qs[:, 2048 + i * 128 : 2048 + (i + 1) * 128]
            wq12[i * 16 : (i + 1) * 16, 128:256] = qs[:, 4096 + i * 128 : 4096 + (i + 1) * 128]
        loads["pa"].wait()
        loads["pb"].wait()
        at = iota((256, 64), 0) - iota((256, 64), 1)
        pbt1[...] = nn((at == 0).astype(F32).astype(BF16), pb[...]).astype(BF16)
        pbt2[...] = nn((at == 64).astype(F32).astype(BF16), pb[...]).astype(BF16)
        at = iota((256, 32), 0) - iota((256, 32), 1)
        pat[...] = nn((at == 128).astype(F32).astype(BF16), pa[...]).astype(BF16)

    def send_weights():
        for pos in range(NZ):
            if pos == LOCAL:
                remote(
                    wrow.at[2 * pos + other],
                    wrecv.at[2 * pos + c],
                    w_send,
                    w_recv,
                    device(y, z * 2 + other, x),
                )
                wrecv[2 * pos + c] = wrow[2 * pos + c]
            else:
                for core in range(2):
                    remote(
                        wrow.at[2 * pos + core],
                        wrecv.at[2 * pos + c],
                        w_send,
                        w_recv,
                        column(pos, core),
                    )

    chip_rows()
    slot_weights()
    send_far(2, 3)
    step_a(0)
    send_far(4)
    send_pair()
    send_near()
    send_weights()
    constants()
    step_b(0)
    step_a(1)
    step_c(0)
    step_d(0, 0)
    step_a(2)
    step_b(1)
    step_d(0, 1, 2)
    step_c(1)
    step_d(0, 3)
    step_b(2)
    for name in ("pin", "pout", "wg", "wu", "wd"):
        loads[name].wait()
    chunks(0, 0, True)
    step_d(1, 0)
    step_d(1, 1, 2)
    step_d(1, 3)
    chunks(0, 1, False)
    step_c(2)
    step_d(2, 0)
    chunks(0, 3, False)
    step_d(2, 1, 2)
    step_d(2, 3)
    step_e(0)
    step_e(1)
    chunks(0, 2, False)
    activations(0)
    scatter(0)
    arrived(full.at[:, :, 2 * NEAR : 2 * NEAR + 4], near_recv)
    arrived(full.at[:, :, 2 * LOCAL + other], pair_recv)
    chunks(1, 0, True)
    chunks(1, 1, False)
    chunks(1, 3, False)
    step_e(2)
    chunks(1, 2, False)
    activations(1)
    scatter(1)
    arrived(wrecv.at[0:15], w_recv)
    local_terms(0)
    gather(0)
    local_terms(1)
    gather(1)
    total0 = scores(0)
    total = total0 + scores(1)

    on_diagonal = iota((16, 128), 0) == iota((16, 128), 1)
    row = jnp.sum(jnp.where(on_diagonal, total, 0.0), axis=0, keepdims=True)
    tot_send[...] = row
    tot_recv[2 * LOCAL + c] = row
    for pos in range(NZ):
        for core in range(2):
            if pos != LOCAL:
                remote(tot_send, tot_recv.at[2 * pos + c], t_send, t_recv, back_column(pos, core))
    remote(
        tot_send,
        tot_recv.at[2 * LOCAL + c],
        t_send,
        t_recv,
        device(y, z * 2 + other, x),
    )

    arrived(score_recv.at[0:15], sc_recv)
    every = jnp.concatenate([score_recv[k] for k in range(16)], axis=1)
    high, low = split(every)
    tok_ref[...] = nn(high, wm_hi[...]) + nn(high, wm_lo[...]) + nn(low, wm_hi[...])
    arrived(tot_recv.at[0:15], t_recv)
    row = tot_recv[0]
    for k in range(1, 16):
        row = row + tot_recv[k]
    tot_ref[...] = row[:, :16] * (1.0 / math.sqrt(2048.0))
    left(full.at[:, 0:9, 0:10], z_send)
    left(full.at[:, 0:15, 0:10], g_send)
    left(wrecv.at[0:15], w_send)
    for cg in range(2):
        left(part.at[cg, 0:15], rs_send.at[cg])
        left(factors.at[cg, 0:15], ag_send.at[cg])
    left(score_recv.at[0:15], sc_send)
    left(tot_recv.at[0:15], t_send)


def body(inputs, cotangents, routes, gates, w_gate, w_up, w_down, proj_in, proj_out, proj_hid_a, proj_hid_b, queries):
    anywhere = pl.BlockSpec(memory_space=pl.ANY)
    vmem = pl.BlockSpec(memory_space=pltpu.VMEM)
    scores, totals = pl.pallas_call(
        kernel,
        out_shape=(jax.ShapeDtypeStruct((16, 128), F32), jax.ShapeDtypeStruct((1, 16), F32)),
        in_specs=[anywhere] * 12,
        out_specs=(vmem, vmem),
        scratch_shapes=[
            pltpu.VMEM((128, 4096), BF16),
            pltpu.VMEM((128, 4096), BF16),
            pltpu.VMEM((2, 128), I32),
            pltpu.VMEM((2, 128), F32),
            pltpu.VMEM((512, 4096), BF16),
            pltpu.VMEM((448, 4096), BF16),
            pltpu.VMEM((512, 4096), BF16),
            pltpu.VMEM((32, 448), BF16),
            pltpu.VMEM((64, 448), BF16),
            pltpu.VMEM((16, 6144), BF16),
            pltpu.VMEM((2, SHARES, 16, SLOTS, COLS), BF16),
            pltpu.VMEM((2, 10, SLOTS, COLS), BF16),
            pltpu.VMEM((2, SHARES, SLOTS, COLS), BF16),
            pltpu.VMEM((2, 4, SHARES, SLOTS, COLS), BF16),
            pltpu.VMEM((2, 256, 512), F32),
            pltpu.VMEM((2, 256, 448), F32),
            pltpu.VMEM((2, 256, 512), F32),
            pltpu.VMEM((2, 4, 256, 256), F32),
            pltpu.VMEM((256, 448), BF16),
            pltpu.VMEM((256, 448), BF16),
            pltpu.VMEM((256, 448), BF16),
            pltpu.VMEM((256, 128), BF16),
            pltpu.VMEM((256, 256), BF16),
            pltpu.VMEM((2048, 128), BF16),
            pltpu.VMEM((2048, 128), BF16),
            pltpu.VMEM((16, 1, 128), F32),
            pltpu.VMEM((16, 1, 128), F32),
            pltpu.VMEM((2, 16, 16, 256), BF16),
            pltpu.VMEM((2, 16, 16, 256), BF16),
            pltpu.VMEM((2, 16, 256), BF16),
            pltpu.VMEM((2, 16, 16, 256), BF16),
            pltpu.VMEM((2, 2, 16, 128), F32),
            pltpu.VMEM((16, 16, 128), F32),
            pltpu.VMEM((1, 128), F32),
            pltpu.VMEM((16, 1, 128), F32),
            pltpu.SemaphoreType.DMA((12,)),
            pltpu.SemaphoreType.DMA,
            pltpu.SemaphoreType.DMA((3, 2)),
            pltpu.SemaphoreType.DMA,
            pltpu.SemaphoreType.DMA,
            pltpu.SemaphoreType.DMA,
            pltpu.SemaphoreType.DMA,
            pltpu.SemaphoreType.DMA,
            pltpu.SemaphoreType.DMA((3, 2, 11)),
            pltpu.SemaphoreType.DMA((3,)),
            pltpu.SemaphoreType.DMA((2,)),
            pltpu.SemaphoreType.DMA((2,)),
            pltpu.SemaphoreType.DMA((2,)),
            pltpu.SemaphoreType.DMA((2,)),
            pltpu.SemaphoreType.DMA,
            pltpu.SemaphoreType.DMA,
            pltpu.SemaphoreType.DMA,
            pltpu.SemaphoreType.DMA,
        ],
        compiler_params=pltpu.CompilerParams(
            collective_id=0, has_side_effects=True, vmem_limit_bytes=60 * 1024 * 1024
        ),
    )(
        inputs,
        cotangents,
        routes.T,
        gates.T,
        w_gate[0].T,
        w_up[0].T,
        w_down[0],
        proj_in.T,
        proj_out.T,
        proj_hid_a.T,
        proj_hid_b.T,
        queries,
    )
    return scores.T, totals.reshape(16)


def solution(mesh):
    placed = (
        P("expert", None),
        P("expert", None),
        P("expert", None),
        P("expert", None),
        P("expert", None, ("dp", "pipe")),
        P("expert", None, ("dp", "pipe")),
        P("expert", ("dp", "pipe"), None),
        P(),
        P(),
        P(("dp", "pipe"), None),
        P(("dp", "pipe"), None),
        P(("dp", "pipe"), None),
    )
    return jax.shard_map(
        body,
        mesh=mesh,
        in_specs=placed,
        out_specs=(P("expert", ("dp", "pipe")), P(("dp", "pipe"))),
        check_vma=False,
    )
```

time: 94.2 us -> 73.6 us (0.78)
  Pallas kernels: 90.9 us -> 70.4 us
    pallas_call x1, Pallas kernels: 90.9 us -> 70.4 us  [body(): pl.pallas_call(kernel, out_shape=(jax.ShapeDtypeStruct((16, 128), F32), j...]
where the time goes in v2:
time: 73.6 us; the launch traced here: 73.5 us
  Pallas kernels  70.4 us (96%)
  local copies, waits for them, and re-layouts  2.43 us (3%)
    pallas_call x1, Pallas kernels, body(): pl.pallas_call(kernel, out_shape=(jax.ShapeDtypeStruct((16, 128), F32), j...  70.4 us
    unnamed x2, local copies, waits for them, and re-layouts  2.43 us

profile of v2, /device:TPU:1, one launch (start us, length us, event | category | flops | bytes accessed | tf_op | source)
XLA Modules:
  0.0 73.5 jit_solution(712961660633935343)
XLA Ops:
  0.6 70.4 %shard_map.131 = (f32[16,128]{1,0:T(8,128)}, f32[1,16]{1,0:T(1,128)}) custom-call(bf16[128,4096]{1,0:T(8,128)(2,1)} %x_hbm.1, bf16[128,4096]{1,0:T(8,128)(2,1)} %g_hbm.1, s32[2,128]{1,0:T(2,128)} %bitcast.23, f32[2,128]{1,0:T(2,128)} %bitcast.24, bf16[448,4096]{1,0:T(8,128)(2,1)} %bitcast.15, bf16[448,4096]{1,0:T(8,128)(2,1)} %bitcast.16, ...), custom_call_target="tpu_custom_call" | custom-call | tf_op jit(solution)/shard_map/pallas_call | solution.py:525
  71.0 1.3 %copy.16 = f32[128,16]{0,1:T(8,128)} copy(f32[128,16]{0,1:T(8,128)} %bitcast.22) | data formatting | bytes 16384
  72.3 1.1 %copy.17 = f32[16]{0:T(128)} copy(f32[16]{0:T(128)} %bitcast.25) | data formatting | bytes 128

commit v3 on v2

--- a/solution.py
+++ b/solution.py
@@ -13,6 +13,7 @@
 NZ = 8
 ORDER = (2, 6, 3, 5, 4, 0, 1, 7)
 LOCAL = ORDER.index(0)
+FIRST = (0, 1, 2, 3, LOCAL, 6, 7)
 NEAR = 6
 SLOTS = 32
 COLS = 256
@@ -21,8 +22,9 @@
 PIECES = (0, -1, 1, 2)
 PLANE = sorted(
     ((dy, dx) for dy in range(4) for dx in range(4) if dy or dx),
-    key=lambda o: min(o[0], 4 - o[0]) + min(o[1], 4 - o[1]),
+    key=lambda o: -min(o[0], 4 - o[0]) - min(o[1], 4 - o[1]),
 )
+FAR_FIRST = sorted(range(NZ), key=lambda i: -min(ORDER[i], NZ - ORDER[i]))
 
 
 def nn(a, b):
@@ -88,9 +90,9 @@
         ).wait_send()
 
     barrier = pltpu.get_barrier_semaphore()
-    for dy, dx in PLANE:
+    for dy, dx in ((0, 1), (0, 3), (1, 0), (3, 0)):
         pl.semaphore_signal(barrier, inc=1, device_id=plane(dy, dx), device_id_type=MESH)
-    for pos in range(NZ):
+    for pos in FIRST:
         if pos == LOCAL:
             pl.semaphore_signal(barrier, inc=1, device_id=column(pos, other), device_id_type=MESH)
         else:
@@ -151,7 +153,7 @@
         rows = nn(picks, source[:, columns]).astype(BF16)
         out_rows[a] = rows.reshape(10, SLOTS, COLS)
 
-    pl.semaphore_wait(barrier, 30)
+    pl.semaphore_wait(barrier, 17)
 
     def send_far(*positions):
         for pos in positions:
@@ -238,10 +240,14 @@
 
     def step_a(g):
         b, n = GROUPS[g]
+        h = n // 2
         for a in range(2):
             arrived(share_ref(a, 0, 0, b, n), z_recv.at[g, a])
-            for tag, d in ((0, 1), (1, -1)):
-                send_group(a, share_ref(a, 0, 0, b, n), g_recv.at[g, a, tag], 0, d)
+            for tag, first in ((0, b), (1, b + h)):
+                other_half = b + h if tag == 0 else b
+                d = 1 if tag == 0 else -1
+                send_group(a, share_ref(a, 0, 0, first, h), g_recv.at[g, a, tag], 0, d)
+                send_group(a, share_ref(a, 0, 0, other_half, h), g_recv.at[g, a, 11 + tag], 0, d)
         if g == 0:
             for a in range(2):
                 send_piece(g, a, 0)
@@ -250,11 +256,13 @@
         b, n = GROUPS[g]
         h = n // 2
         for a in range(2):
-            arrived(share_ref(a, 0, -1, b, n), g_recv.at[g, a, 0])
+            arrived(share_ref(a, 0, -1, b, h), g_recv.at[g, a, 0])
             send_group(a, share_ref(a, 0, -1, b, h), g_recv.at[g, a, 2], 0, 1)
-            arrived(share_ref(a, 0, 1, b, n), g_recv.at[g, a, 1])
+            arrived(share_ref(a, 0, 1, b + h, h), g_recv.at[g, a, 1])
             send_group(a, share_ref(a, 0, 1, b + h, h), g_recv.at[g, a, 2], 0, -1)
         for a in range(2):
+            arrived(share_ref(a, 0, -1, b + h, h), g_recv.at[g, a, 11])
+            arrived(share_ref(a, 0, 1, b, h), g_recv.at[g, a, 12])
             for piece in (1, 2) if g == 0 else (0, 1, 2):
                 send_piece(g, a, piece)
 
@@ -433,13 +441,13 @@
 
     chip_rows()
     slot_weights()
+    constants()
     send_far(2, 3)
     step_a(0)
     send_far(4)
     send_pair()
     send_near()
     send_weights()
-    constants()
     step_b(0)
     step_a(1)
     step_c(0)
@@ -461,15 +469,15 @@
     step_d(2, 0)
     chunks(0, 3, False)
     step_d(2, 1, 2)
+    arrived(full.at[:, :, 2 * NEAR : 2 * NEAR + 4], near_recv)
+    arrived(full.at[:, :, 2 * LOCAL + other], pair_recv)
+    chunks(1, 0, True)
     step_d(2, 3)
     step_e(0)
     step_e(1)
     chunks(0, 2, False)
     activations(0)
     scatter(0)
-    arrived(full.at[:, :, 2 * NEAR : 2 * NEAR + 4], near_recv)
-    arrived(full.at[:, :, 2 * LOCAL + other], pair_recv)
-    chunks(1, 0, True)
     chunks(1, 1, False)
     chunks(1, 3, False)
     step_e(2)
@@ -488,7 +496,7 @@
     row = jnp.sum(jnp.where(on_diagonal, total, 0.0), axis=0, keepdims=True)
     tot_send[...] = row
     tot_recv[2 * LOCAL + c] = row
-    for pos in range(NZ):
+    for pos in FAR_FIRST:
         for core in range(2):
             if pos != LOCAL:
                 remote(tot_send, tot_recv.at[2 * pos + c], t_send, t_recv, back_column(pos, core))
@@ -508,7 +516,7 @@
     row = tot_recv[0]
     for k in range(1, 16):
         row = row + tot_recv[k]
-    tot_ref[...] = row[:, :16] * (1.0 / math.sqrt(2048.0))
+    tot_ref[...] = row[:, :16]
     left(full.at[:, 0:9, 0:10], z_send)
     left(full.at[:, 0:15, 0:10], g_send)
     left(wrecv.at[0:15], w_send)
@@ -517,6 +525,11 @@
         left(factors.at[cg, 0:15], ag_send.at[cg])
     left(score_recv.at[0:15], sc_send)
     left(tot_recv.at[0:15], t_send)
+
+
+def results(scores_ref, totals_ref, scores_out, totals_out):
+    scores_out[...] = scores_ref[...]
+    totals_out[...] = totals_ref[...] * (1.0 / math.sqrt(2048.0))
 
 
 def body(inputs, cotangents, routes, gates, w_gate, w_up, w_down, proj_in, proj_out, proj_hid_a, proj_hid_b, queries):
@@ -571,7 +584,7 @@
             pltpu.SemaphoreType.DMA,
             pltpu.SemaphoreType.DMA,
             pltpu.SemaphoreType.DMA,
-            pltpu.SemaphoreType.DMA((3, 2, 11)),
+            pltpu.SemaphoreType.DMA((3, 2, 13)),
             pltpu.SemaphoreType.DMA((3,)),
             pltpu.SemaphoreType.DMA((2,)),
             pltpu.SemaphoreType.DMA((2,)),
@@ -599,6 +612,10 @@
         proj_hid_b.T,
         queries,
     )
+    scores, totals = pl.pallas_call(
+        results,
+        out_shape=(jax.ShapeDtypeStruct((16, 128), F32), jax.ShapeDtypeStruct((1, 16), F32)),
+    )(scores, totals)
     return scores.T, totals.reshape(16)
 
 

time: 73.6 us -> 69.1 us (0.939)
  local copies, waits for them, and re-layouts: 2.43 us -> 0 us
  Pallas kernels: 70.4 us -> 68.3 us
    pallas_call x1, Pallas kernels: 70.4 us -> 67 us  [body(): pl.pallas_call(kernel, out_shape=(jax.ShapeDtypeStruct((16, 128), F32), j...]
    unnamed x2 -> x0, local copies, waits for them, and re-layouts: 2.43 us -> none
    pallas_call x0 -> x1, Pallas kernels: none -> 1.3 us  [body(): pl.pallas_call(results, out_shape=(jax.ShapeDtypeStruct((16, 128), F32),...]
where the time goes in v3:
time: 69.1 us; the launch traced here: 69 us
  Pallas kernels  68.3 us (99%)
    pallas_call x1, Pallas kernels, body(): pl.pallas_call(kernel, out_shape=(jax.ShapeDtypeStruct((16, 128), F32), j...  67 us

profile of v3, /device:TPU:1, one launch (start us, length us, event | category | flops | bytes accessed | tf_op | source)
XLA Modules:
  0.0 69.0 jit_solution(4931770014496558971)
XLA Ops:
  0.6 67.0 %shard_map.131 = (f32[16,128]{1,0:T(8,128)}, f32[1,16]{1,0:T(1,128)}) custom-call(bf16[128,4096]{1,0:T(8,128)(2,1)} %x_hbm.1, bf16[128,4096]{1,0:T(8,128)(2,1)} %g_hbm.1, s32[2,128]{1,0:T(2,128)} %bitcast.22, f32[2,128]{1,0:T(2,128)} %bitcast.23, bf16[448,4096]{1,0:T(8,128)(2,1)} %bitcast.15, bf16[448,4096]{1,0:T(8,128)(2,1)} %bitcast.16, ...), custom_call_target="tpu_custom_call" | custom-call | tf_op jit(solution)/shard_map/pallas_call | solution.py:538
  67.7 1.3 %shard_map.132 = (f32[16,128]{1,0:T(8,128)}, f32[1,16]{1,0:T(1,128)}) custom-call(f32[16,128]{1,0:T(8,128)} %get-tuple-element.6.scores_ref, f32[1,16]{1,0:T(1,128)} %get-tuple-element.7.totals_ref), custom_call_target="tpu_custom_call" | custom-call | tf_op jit(solution)/shard_map/pallas_call | solution.py:615

commit v4 on v3

--- a/solution.py
+++ b/solution.py
@@ -13,7 +13,7 @@
 NZ = 8
 ORDER = (2, 6, 3, 5, 4, 0, 1, 7)
 LOCAL = ORDER.index(0)
-FIRST = (0, 1, 2, 3, LOCAL, 6, 7)
+FIRST = (0, 1, LOCAL, 6, 7)
 NEAR = 6
 SLOTS = 32
 COLS = 256
@@ -53,6 +53,7 @@
     part, gathered, own, factors, score_send, score_recv, tot_send, tot_recv,
     load_sem, z_send, z_recv, pair_recv, near_recv, w_send, w_recv,
     g_send, g_recv, e_recv, rs_send, rs_recv, ag_send, ag_recv, sc_send, sc_recv, t_send, t_recv,
+    passed,
 ):
     y, e, x = lax.axis_index("dp"), lax.axis_index("expert"), lax.axis_index("pipe")
     z, c = lax.div(e, 2), lax.rem(e, 2)
@@ -153,7 +154,7 @@
         rows = nn(picks, source[:, columns]).astype(BF16)
         out_rows[a] = rows.reshape(10, SLOTS, COLS)
 
-    pl.semaphore_wait(barrier, 17)
+    pl.semaphore_wait(barrier, 13)
 
     def send_far(*positions):
         for pos in positions:
@@ -168,6 +169,9 @@
                     )
 
     send_far(0, 1)
+    for pos in range(NEAR, NZ):
+        for core in range(2):
+            pl.semaphore_signal(passed, inc=1, device_id=column(pos, core), device_id_type=MESH)
 
     near_picks = picks_of(2 * NEAR * SLOTS, 4 * SLOTS)
     for a, source in enumerate((xs, gs)):
@@ -442,6 +446,7 @@
     chip_rows()
     slot_weights()
     constants()
+    pl.semaphore_wait(passed, 4)
     send_far(2, 3)
     step_a(0)
     send_far(4)
@@ -455,31 +460,31 @@
     step_a(2)
     step_b(1)
     step_d(0, 1, 2)
+    step_b(2)
     step_c(1)
     step_d(0, 3)
-    step_b(2)
     for name in ("pin", "pout", "wg", "wu", "wd"):
         loads[name].wait()
     chunks(0, 0, True)
     step_d(1, 0)
     step_d(1, 1, 2)
+    step_c(2)
+    step_d(2, 0)
+    step_d(2, 1, 2)
     step_d(1, 3)
     chunks(0, 1, False)
-    step_c(2)
-    step_d(2, 0)
     chunks(0, 3, False)
-    step_d(2, 1, 2)
     arrived(full.at[:, :, 2 * NEAR : 2 * NEAR + 4], near_recv)
     arrived(full.at[:, :, 2 * LOCAL + other], pair_recv)
     chunks(1, 0, True)
     step_d(2, 3)
+    chunks(1, 1, False)
+    chunks(1, 3, False)
     step_e(0)
     step_e(1)
     chunks(0, 2, False)
     activations(0)
     scatter(0)
-    chunks(1, 1, False)
-    chunks(1, 3, False)
     step_e(2)
     chunks(1, 2, False)
     activations(1)
@@ -594,6 +599,7 @@
             pltpu.SemaphoreType.DMA,
             pltpu.SemaphoreType.DMA,
             pltpu.SemaphoreType.DMA,
+            pltpu.SemaphoreType.REGULAR,
         ],
         compiler_params=pltpu.CompilerParams(
             collective_id=0, has_side_effects=True, vmem_limit_bytes=60 * 1024 * 1024

time: 69.1 us -> 67.9 us (0.983)
  Pallas kernels: 68.3 us -> 67.1 us
    pallas_call x1, Pallas kernels: 67 us -> 65.8 us  [body(): pl.pallas_call(kernel, out_shape=(jax.ShapeDtypeStruct((16, 128), F32), j...]
where the time goes in v4:
time: 67.9 us; the launch traced here: 67.7 us
  Pallas kernels  67.1 us (99%)
    pallas_call x1, Pallas kernels, body(): pl.pallas_call(kernel, out_shape=(jax.ShapeDtypeStruct((16, 128), F32), j...  65.8 us

profile of v4, /device:TPU:1, one launch (start us, length us, event | category | flops | bytes accessed | tf_op | source)
XLA Modules:
  0.0 67.7 jit_solution(14954287812949499184)
XLA Ops:
  0.6 65.8 %shard_map.131 = (f32[16,128]{1,0:T(8,128)}, f32[1,16]{1,0:T(1,128)}) custom-call(bf16[128,4096]{1,0:T(8,128)(2,1)} %x_hbm.1, bf16[128,4096]{1,0:T(8,128)(2,1)} %g_hbm.1, s32[2,128]{1,0:T(2,128)} %bitcast.22, f32[2,128]{1,0:T(2,128)} %bitcast.23, bf16[448,4096]{1,0:T(8,128)(2,1)} %bitcast.15, bf16[448,4096]{1,0:T(8,128)(2,1)} %bitcast.16, ...), custom_call_target="tpu_custom_call" | custom-call | tf_op jit(solution)/shard_map/pallas_call | solution.py:543
  66.4 1.3 %shard_map.132 = (f32[16,128]{1,0:T(8,128)}, f32[1,16]{1,0:T(1,128)}) custom-call(f32[16,128]{1,0:T(8,128)} %get-tuple-element.6.scores_ref, f32[1,16]{1,0:T(1,128)} %get-tuple-element.7.totals_ref), custom_call_target="tpu_custom_call" | custom-call | tf_op jit(solution)/shard_map/pallas_call | solution.py:621

commit v5 on v4

--- a/solution.py
+++ b/solution.py
@@ -49,7 +49,7 @@
     tok_ref, tot_ref,
     xs, gs, routes, gates, wg, wu, wd, pa, pb, qs,
     full, out_rows, out_pair, out_near, acc0, acc1, acc2, terms,
-    pat, pbt1, pbt2, wq0, wq12, wm_hi, wm_lo, wrow, wrecv,
+    pat0, pat1, pbt1, pbt2, wq0, wq12, wm_hi, wm_lo, wrow, wrecv,
     part, gathered, own, factors, score_send, score_recv, tot_send, tot_recv,
     load_sem, z_send, z_recv, pair_recv, near_recv, w_send, w_recv,
     g_send, g_recv, e_recv, rs_send, rs_recv, ag_send, ag_recv, sc_send, sc_recv, t_send, t_recv,
@@ -317,8 +317,10 @@
         hidden = (gated * up).astype(BF16)
         d_up = (back * gated).astype(BF16)
         d_gate = (back * up * s * (1.0 + gate * (1.0 - s))).astype(BF16)
-        sums = nt(d_up, pbt1[...]) + nt(d_gate, pbt2[...]) + nt(hidden, pat[...])
-        part[cg] = sums.astype(BF16).reshape(16, 16, 256)
+        grads = nt(d_up, pbt1[...]) + nt(d_gate, pbt2[...])
+        halves = nt(hidden[0:128], pat0[...]) + nt(hidden[128:256], pat1[...])
+        part[cg, :, 0:16] = grads.reshape(16, 16, 128).astype(BF16)
+        part[cg, :, 16:24] = halves.reshape(16, 8, 128).astype(BF16)
 
     def scatter(cg):
         for dy, dx in PLANE:
@@ -364,16 +366,19 @@
 
     def scores(cg):
         arrived(factors.at[cg, 0:15], ag_recv.at[cg])
-        all_rows = factors[cg].reshape(256, 256)
-        b_both = all_rows[:, :128].astype(F32)
+        b_both = factors[cg, :, 0:16].reshape(256, 128).astype(F32)
         b_turned = pltpu.roll(b_both, 64, 1)
-        a_hidden = all_rows[:, 128:]
+        a_hidden = factors[cg, :, 16:24].astype(F32).reshape(128, 128).astype(BF16)
+
+        def hidden_spread(odd):
+            return jnp.concatenate([nn(a_hidden, picked(0, odd)), nn(a_hidden, picked(32, odd))], axis=0)
+
         even = jnp.concatenate([jnp.where(low_half, b_both, 0.0), jnp.where(low_half, b_turned, 0.0)], axis=1)
         odd = jnp.concatenate([jnp.where(low_half, 0.0, b_turned), jnp.where(low_half, 0.0, b_both)], axis=1)
         z_sum = terms[cg, 0] * nt(even.astype(BF16), wq12[...])
         z_sum += terms[cg, 1] * nt(odd.astype(BF16), wq12[...])
-        z_sum += nn(a_hidden, picked(0, 0)) * terms[cg, 2]
-        z_sum += nn(a_hidden, picked(0, 1)) * terms[cg, 3]
+        z_sum += hidden_spread(0) * terms[cg, 2]
+        z_sum += hidden_spread(1) * terms[cg, 3]
         high, low = split(z_sum)
         fold = (lax.rem(iota((16, 256), 1), 16) == iota((16, 256), 0)).astype(F32).astype(BF16)
         score = nt(fold, high) + nt(fold, low)
@@ -416,11 +421,12 @@
             wq12[i * 16 : (i + 1) * 16, 128:256] = qs[:, 4096 + i * 128 : 4096 + (i + 1) * 128]
         loads["pa"].wait()
         loads["pb"].wait()
-        at = iota((256, 64), 0) - iota((256, 64), 1)
+        at = iota((128, 64), 0) - iota((128, 64), 1)
         pbt1[...] = nn((at == 0).astype(F32).astype(BF16), pb[...]).astype(BF16)
         pbt2[...] = nn((at == 64).astype(F32).astype(BF16), pb[...]).astype(BF16)
-        at = iota((256, 32), 0) - iota((256, 32), 1)
-        pat[...] = nn((at == 128).astype(F32).astype(BF16), pa[...]).astype(BF16)
+        at = iota((128, 32), 0) - iota((128, 32), 1)
+        pat0[...] = nn((at == 0).astype(F32).astype(BF16), pa[...]).astype(BF16)
+        pat1[...] = nn((at == 32).astype(F32).astype(BF16), pa[...]).astype(BF16)
 
     def send_weights():
         for pos in range(NZ):
@@ -564,19 +570,20 @@
             pltpu.VMEM((2, 256, 448), F32),
             pltpu.VMEM((2, 256, 512), F32),
             pltpu.VMEM((2, 4, 256, 256), F32),
-            pltpu.VMEM((256, 448), BF16),
-            pltpu.VMEM((256, 448), BF16),
-            pltpu.VMEM((256, 448), BF16),
+            pltpu.VMEM((128, 448), BF16),
+            pltpu.VMEM((128, 448), BF16),
+            pltpu.VMEM((128, 448), BF16),
+            pltpu.VMEM((128, 448), BF16),
             pltpu.VMEM((256, 128), BF16),
             pltpu.VMEM((256, 256), BF16),
             pltpu.VMEM((2048, 128), BF16),
             pltpu.VMEM((2048, 128), BF16),
             pltpu.VMEM((16, 1, 128), F32),
             pltpu.VMEM((16, 1, 128), F32),
-            pltpu.VMEM((2, 16, 16, 256), BF16),
-            pltpu.VMEM((2, 16, 16, 256), BF16),
-            pltpu.VMEM((2, 16, 256), BF16),
-            pltpu.VMEM((2, 16, 16, 256), BF16),
+            pltpu.VMEM((2, 16, 24, 128), BF16),
+            pltpu.VMEM((2, 16, 24, 128), BF16),
+            pltpu.VMEM((2, 24, 128), BF16),
+            pltpu.VMEM((2, 16, 24, 128), BF16),
             pltpu.VMEM((2, 2, 16, 128), F32),
             pltpu.VMEM((16, 16, 128), F32),
             pltpu.VMEM((1, 128), F32),

time: 67.9 us -> 67 us (0.987)
  Pallas kernels: 67.1 us -> 66.1 us
    pallas_call x1, Pallas kernels: 65.8 us -> 64.8 us  [body(): pl.pallas_call(kernel, out_shape=(jax.ShapeDtypeStruct((16, 128), F32), j...]
where the time goes in v5:
time: 67 us; the launch traced here: 66.8 us
  Pallas kernels  66.1 us (99%)
    pallas_call x1, Pallas kernels, body(): pl.pallas_call(kernel, out_shape=(jax.ShapeDtypeStruct((16, 128), F32), j...  64.8 us

profile of v5, /device:TPU:1, one launch (start us, length us, event | category | flops | bytes accessed | tf_op | source)
XLA Modules:
  0.0 66.8 jit_solution(1591337070701136617)
XLA Ops:
  0.6 64.8 %shard_map.131 = (f32[16,128]{1,0:T(8,128)}, f32[1,16]{1,0:T(1,128)}) custom-call(bf16[128,4096]{1,0:T(8,128)(2,1)} %x_hbm.1, bf16[128,4096]{1,0:T(8,128)(2,1)} %g_hbm.1, s32[2,128]{1,0:T(2,128)} %bitcast.22, f32[2,128]{1,0:T(2,128)} %bitcast.23, bf16[448,4096]{1,0:T(8,128)(2,1)} %bitcast.15, bf16[448,4096]{1,0:T(8,128)(2,1)} %bitcast.16, ...), custom_call_target="tpu_custom_call" | custom-call | tf_op jit(solution)/shard_map/pallas_call | solution.py:549
  65.5 1.3 %shard_map.132 = (f32[16,128]{1,0:T(8,128)}, f32[1,16]{1,0:T(1,128)}) custom-call(f32[16,128]{1,0:T(8,128)} %get-tuple-element.6.scores_ref, f32[1,16]{1,0:T(1,128)} %get-tuple-element.7.totals_ref), custom_call_target="tpu_custom_call" | custom-call | tf_op jit(solution)/shard_map/pallas_call | solution.py:628

commit v6 on v5

--- a/solution.py
+++ b/solution.py
@@ -392,7 +392,7 @@
                         tile,
                         score_recv.at[2 * pos + c],
                         sc_send,
-                        sc_recv,
+                        sc_recv.at[cg],
                         back_column(pos, core),
                     )
             if pos == LOCAL:
@@ -400,7 +400,7 @@
                     tile,
                     score_recv.at[2 * pos + c],
                     sc_send,
-                    sc_recv,
+                    sc_recv.at[cg],
                     device(y, z * 2 + other, x),
                 )
                 score_recv[2 * pos + c] = score_send[cg, (pos % 4) // 2]
@@ -519,10 +519,16 @@
         device(y, z * 2 + other, x),
     )
 
-    arrived(score_recv.at[0:15], sc_recv)
-    every = jnp.concatenate([score_recv[k] for k in range(16)], axis=1)
-    high, low = split(every)
-    tok_ref[...] = nn(high, wm_hi[...]) + nn(high, wm_lo[...]) + nn(low, wm_hi[...])
+    def combined(first):
+        every = jnp.concatenate([score_recv[k] for k in range(first, first + 8)], axis=1)
+        high, low = split(every)
+        slots = pl.ds(first * 128, 1024)
+        return nn(high, wm_hi[slots]) + nn(high, wm_lo[slots]) + nn(low, wm_hi[slots])
+
+    arrived(score_recv.at[0:8], sc_recv.at[0])
+    tok_ref[...] = combined(0)
+    arrived(score_recv.at[8:15], sc_recv.at[1])
+    tok_ref[...] = tok_ref[...] + combined(8)
     arrived(tot_recv.at[0:15], t_recv)
     row = tot_recv[0]
     for k in range(1, 16):
@@ -603,7 +609,7 @@
             pltpu.SemaphoreType.DMA((2,)),
             pltpu.SemaphoreType.DMA((2,)),
             pltpu.SemaphoreType.DMA,
-            pltpu.SemaphoreType.DMA,
+            pltpu.SemaphoreType.DMA((2,)),
             pltpu.SemaphoreType.DMA,
             pltpu.SemaphoreType.DMA,
             pltpu.SemaphoreType.REGULAR,

time: 67 us -> 66.8 us (level)
  no operation moved by 1% of the time
where the time goes in v6:
time: 66.8 us; the launch traced here: 66.6 us
  Pallas kernels  66 us (99%)
    pallas_call x1, Pallas kernels, body(): pl.pallas_call(kernel, out_shape=(jax.ShapeDtypeStruct((16, 128), F32), j...  64.7 us

profile of v6, /device:TPU:1, one launch (start us, length us, event | category | flops | bytes accessed | tf_op | source)
XLA Modules:
  0.0 66.6 jit_solution(11071517991445042105)
XLA Ops:
  0.6 64.7 %shard_map.131 = (f32[16,128]{1,0:T(8,128)}, f32[1,16]{1,0:T(1,128)}) custom-call(bf16[128,4096]{1,0:T(8,128)(2,1)} %x_hbm.1, bf16[128,4096]{1,0:T(8,128)(2,1)} %g_hbm.1, s32[2,128]{1,0:T(2,128)} %bitcast.22, f32[2,128]{1,0:T(2,128)} %bitcast.23, bf16[448,4096]{1,0:T(8,128)(2,1)} %bitcast.15, bf16[448,4096]{1,0:T(8,128)(2,1)} %bitcast.16, ...), custom_call_target="tpu_custom_call" | custom-call | tf_op jit(solution)/shard_map/pallas_call | solution.py:555
  65.3 1.3 %shard_map.132 = (f32[16,128]{1,0:T(8,128)}, f32[1,16]{1,0:T(1,128)}) custom-call(f32[16,128]{1,0:T(8,128)} %get-tuple-element.6.scores_ref, f32[1,16]{1,0:T(1,128)} %get-tuple-element.7.totals_ref), custom_call_target="tpu_custom_call" | custom-call | tf_op jit(solution)/shard_map/pallas_call | solution.py:634
